TPU v7x, 128 devices: a whole 4x4x4 slice. The times are simulated.
128 devices in a mesh: hst: 8 (over y, core), dev: 16 (over z, x).
Axes of the slice: x: 4, y: 4, z: 4, core: 2. Of those that a mesh axis runs over, the one named last changes fastest.
Arguments:
- hot_rows: bfloat16 [4096, 768], replicated, may hold values from -6 to 6
- cold_rows: bfloat16 [131072, 768], P(('hst', 'dev')), may hold values from -6 to 6
- hot_mask: int32 [262144], P(('hst', 'dev')), may hold values from 0 to 1, as said below
- hot_id: int32 [262144], P(('hst', 'dev')), may hold values from 0 to 4095
- cold_owner: int32 [262144], P(('hst', 'dev')), may hold values from 0 to 127, as said below
- cold_pos: int32 [262144], P(('hst', 'dev')), may hold values from 0 to 15, as said below
- cold_send: int32 [128, 2048], P(('hst', 'dev')), may hold values from 0 to 1023
- adjacency_one: int32 [262144, 15], P(('hst', 'dev')), may hold values from 0 to 2047
- adjacency_two: int32 [65536, 15], P(('hst', 'dev')), may hold values from 0 to 2559
- halo_send: int32 [128, 512], P(('hst', 'dev')), may hold values from 0 to 2047
- self_first: bfloat16 [768, 1024], replicated, may hold values from -0.21875 to 0.21875
- neigh_first: bfloat16 [768, 1024], replicated, may hold values from -0.21875 to 0.21875
- bn_gain: float32 [1024], replicated, may hold values from 0.1 to 1.9
- bn_shift: float32 [1024], replicated, may hold values from -3 to 3
- self_second: bfloat16 [1024, 153], replicated, may hold values from -0.1875 to 0.1875
- neigh_second: bfloat16 [1024, 153], replicated, may hold values from -0.1875 to 0.1875
Outputs:
- logits: float32 [65536, 153], P(('hst', 'dev'))
Inputs may be any that keep to these rules, and one draw needn't show every extreme that they name: Each device has exactly 1536 nodes with hot_mask 0. `cold_owner`: for each device and owner, at most 16 of the device's nodes with hot_mask 0 name that owner; some owner is named by exactly 16 of them on every device. `cold_pos`: the nodes of one device with hot_mask 0 and the same owner have distinct slots.
All inputs are finite; a program needn't handle non-finite values.
Results may differ from a plain program's by a relative error of at most 0.003.
The roundings to bfloat16 on the way count: a program that leaves them out, or rounds other values in their place, can miss the bound.
Values may be sent and summed in bfloat16 or wider, within the bound.
No kernel may reach another device: no remote copies, remote signals or barrier semaphores. Data moves between devices by JAX's collectives and lax.ppermute only.
A program may use at most 128 MiB of HBM per device.

v0:
```python
import functools

import jax
import jax.numpy as jnp
from jax import lax
from jax.sharding import Mesh
from jax.sharding import PartitionSpec as P

HST = ("hst_0", "hst_1")
DEV = ("dev_0", "dev_1")
HST_DEV = ("hst_0", "hst_1", "dev_0", "dev_1")


epsilon = 1e-05


def one_axis_at_a_time(array, axes):
    return functools.reduce(lax.psum, axes, array)


def neighbour_mean(table, neighbours, fanout):
    columns = jnp.arange(table.shape[0], dtype=jnp.int32)
    counts = jnp.zeros((neighbours.shape[0], table.shape[0]), jnp.int32)
    for column in range(fanout):
        counts = counts + (neighbours[:, column : column + 1] == columns[None, :]).astype(jnp.int32)
    total = jnp.dot(counts.astype(jnp.bfloat16), table, preferred_element_type=jnp.float32)
    return (total / fanout).astype(jnp.bfloat16)


def local(
    hot_rows,
    cold_rows,
    hot_mask,
    hot_id,
    cold_owner,
    cold_pos,
    cold_send,
    adjacency_one,
    adjacency_two,
    halo_send,
    self_first,
    neigh_first,
    bn_gain,
    bn_shift,
    self_second,
    neigh_second,
):
    hosts = lax.axis_size(HST)
    within = lax.axis_size(DEV)
    outgoing = jnp.take(cold_rows, cold_send[0], axis=0)
    slots = outgoing.shape[0] // (hosts * within)
    arrived = lax.all_to_all(outgoing, HST_DEV, split_axis=0, concat_axis=0, tiled=True)
    cold_feat = jnp.take(arrived, cold_owner * slots + cold_pos, axis=0)
    hot_feat = jnp.take(hot_rows, hot_id, axis=0)
    features = jnp.where(hot_mask[:, None] == 1, hot_feat, cold_feat)
    first_mean = neighbour_mean(features, adjacency_one, adjacency_one.shape[1])
    hidden_pre = jnp.dot(features, self_first, preferred_element_type=jnp.float32) + jnp.dot(
        first_mean, neigh_first, preferred_element_type=jnp.float32
    )
    total_rows = hidden_pre.shape[0] * hosts * within
    sums, squares = (
        one_axis_at_a_time(jnp.sum(hidden_pre, axis=0), HST_DEV),
        one_axis_at_a_time(jnp.sum(hidden_pre * hidden_pre, axis=0), HST_DEV),
    )
    mean = sums / total_rows
    variance = squares / total_rows - mean * mean
    hidden = jax.nn.relu(
        (hidden_pre - mean) * lax.rsqrt(variance + epsilon) * bn_gain + bn_shift
    ).astype(jnp.bfloat16)
    boundary = jnp.take(hidden, halo_send[0], axis=0)
    received = lax.all_to_all(boundary, DEV, split_axis=0, concat_axis=0, tiled=True)
    table = jnp.concatenate([hidden, received], axis=0)
    targets = adjacency_two.shape[0]
    second_mean = neighbour_mean(table, adjacency_two, adjacency_two.shape[1])
    return jnp.dot(hidden[:targets], self_second, preferred_element_type=jnp.float32) + jnp.dot(
        second_mean, neigh_second, preferred_element_type=jnp.float32
    )


def solution(mesh):
    torus = Mesh(mesh.devices.reshape(4, 2, 4, 4), ("hst_0", "hst_1", "dev_0", "dev_1"))
    return jax.shard_map(
        local,
        mesh=torus,
        in_specs=(
            P(),
            P(HST_DEV, None),
            P(HST_DEV),
            P(HST_DEV),
            P(HST_DEV),
            P(HST_DEV),
            P(HST_DEV, None),
            P(HST_DEV, None),
            P(HST_DEV, None),
            P(HST_DEV, None),
            P(),
            P(),
            P(),
            P(),
            P(),
            P(),
        ),
        out_specs=P(HST_DEV, None),
        check_vma=False,
    )
```

profile of v0, /device:TPU:0, one launch (start us, length us, event | category | flops | bytes accessed | tf_op | source)
XLA Modules:
  0.0 229.3 jit_solution(15472571585349009531)
XLA Ops:
  0.0 0.0 copy-start
  0.0 0.8 compare_select_fusion.1
  0.8 0.5 broadcast.108
  1.3 1.4 reduce.6
  2.7 0.1 squeeze.10
  2.8 11.7 %gather_fusion.1 = bf16[2048,768]{1,0:T(8,128)(2,1)} fusion(bf16[1024,768]{1,0:T(8,128)(2,1)} %param.17, s32[2048]{0:T(1024)S(1)} %broadcast_clamp_fusion.1), kind=kCustom, calls=%fused_computation.1 | custom fusion | bytes 6299648 | tf_op jit(solution)/shard_map/jit(_take)/gather | solution.py:50
  14.6 0.0 copy-start.8
  14.6 0.0 copy-start.5
  14.6 3.4 %broadcast_select_fusion = bf16[128,16,768]{2,1,0:T(8,128)(2,1)} fusion(bf16[128,16,768]{2,1,0:T(8,128)(2,1)} %bitcast.44, pred[128,16]{1,0:T(8,128)(4,1)S(1)} %compare_and_fusion), kind=kLoop, calls=%fused_computation.62 | loop fusion | flops 1572864 | bytes 6293504 | tf_op jit(solution)/shard_map/jit(_take)/select_n | solution.py:50
  17.9 11.6 %all-to-all-start = ((bf16[128,16,768]{2,1,0:T(8,128)(2,1)}), bf16[128,16,768]{2,1,0:T(8,128)(2,1)}, u32[]{:S(2)}, u32[]{:S(2)}) async-start(bf16[128,16,768]{2,1,0:T(8,128)(2,1)} %broadcast_select_fusion), calls=%async_computation | async-start | bytes 6291456 | tf_op jit(solution)/shard_map/all_to_all | solution.py:52
  29.6 0.0 copy-done.8
  29.6 0.7 reduce.7
  30.3 0.1 squeeze.12
  30.3 0.0 copy-done.5
  30.3 0.0 copy-start.7
  30.4 0.0 copy-start.3
  30.4 0.0 copy-start.4
  30.4 0.0 copy-start.2
  30.4 13.7 %gather_fusion = bf16[2048,768]{1,0:T(8,128)(2,1)} fusion(bf16[4096,768]{1,0:T(8,128)(2,1)} %param.16, s32[2048]{0:T(1024)S(1)} %fusion.43), kind=kCustom, calls=%fused_computation | custom fusion | bytes 6299648 | tf_op jit(solution)/shard_map/jit(_take)/gather | solution.py:54
  44.1 0.0 copy-done.7
  44.2 0.0 copy-done.3
  44.2 0.0 copy-done.4
  44.2 0.0 copy-done.2
  44.2 0.1 fusion.50
  44.3 25.2 %all-to-all-done = bf16[128,16,768]{2,1,0:T(8,128)(2,1)} async-done(((bf16[128,16,768]{2,1,0:T(8,128)(2,1)}), bf16[128,16,768]{2,1,0:T(8,128)(2,1)}, u32[]{:S(2)}, u32[]{:S(2)}) %all-to-all-start) | async-done | bytes 3145760 | tf_op jit(solution)/shard_map/all_to_all | solution.py:52
  69.6 12.4 %gather_fusion.2 = bf16[2048,768]{1,0:T(8,128)(2,1)} fusion(bf16[2048,768]{1,0:T(8,128)(2,1)} %bitcast.3, s32[2048]{0:T(1024)S(1)} %broadcast_clamp_fusion), kind=kCustom, calls=%fused_computation.2 | custom fusion | bytes 6299648 | tf_op jit(solution)/shard_map/jit(_take)/gather | solution.py:53
  82.0 8.4 %fusion.48 = f32[2048,1024]{1,0:T(8,128)} fusion(bf16[768,1024]{1,0:T(8,128)(2,1)} %param.26, bf16[2048,768]{1,0:T(8,128)(2,1)} %gather_fusion.2, bf16[2048,768]{1,0:T(8,128)(2,1)} %gather_fusion, pred[2048]{0:T(1024)(128)(4,1)S(1)} %get-tuple-element.48, pred[2048]{0:T(1024)(128)(4,1)S(1)} %get-tuple-element.49, pred[2048]{0:T(1024)(128)(4,1)S(1)} %broadcast_compare_fusion), kind=kOutput, calls=%fused_computation.104 | convolution fusion | flops 3225944064 | bytes 16259072 | tf_op jit(solution)/shard_map/dot_general | solution.py:57
  90.4 0.0 copy-done
  90.4 0.0 copy-start.9
  90.4 0.0 copy-start.10
  90.4 60.2 %fusion.49 = (f32[1024]{0:T(1024)S(1)}, f32[1024]{0:T(1024)S(1)}, f32[2048,1024]{1,0:T(8,128)}) fusion(f32[2048,1024]{1,0:T(8,128)} %fusion.48, bf16[768,1024]{1,0:T(8,128)(2,1)S(1)} %copy-done, s32[2048]{0:T(1024)S(1)} %bitcast.61, s32[2048]{0:T(1024)S(1)} %bitcast.62, s32[2048]{0:T(1024)S(1)} %bitcast.49, s32[2048]{0:T(1024)S(1)} %bitcast.50, ...), kind=kOutput, calls=%fused_computation.105 | convolution fusion | flops 9868670976 | bytes 24778752 | tf_op jit(solution)/shard_map/dot_general | solution.py:57
  150.6 9.4 %all-reduce.2 = (f32[1024]{0:T(1024)S(1)}, f32[1024]{0:T(1024)S(1)}) all-reduce(f32[1024]{0:T(1024)S(1)} %get-tuple-element.6, f32[1024]{0:T(1024)S(1)} %get-tuple-element.5), channel_id=1, replica_groups=mesh['hst_0'=4,'hst_1'=2,'dev_0'=4,'dev_1'=4] {'hst_0'}, use_global_device_ids=true, to_apply=%region_6.7 | all-reduce | flops 2048 | bytes 16384 | tf_op jit(solution)/shard_map/psum | solution.py:18
  160.0 2.5 %all-reduce.3 = (f32[1024]{0:T(1024)S(1)}, f32[1024]{0:T(1024)S(1)}) all-reduce(f32[1024]{0:T(1024)S(1)} %get-tuple-element.11, f32[1024]{0:T(1024)S(1)} %get-tuple-element.12), channel_id=1, replica_groups=mesh['hst_0'=4,'hst_1'=2,'dev_0'=4,'dev_1'=4] {'hst_1'}, use_global_device_ids=true, to_apply=%region_7.8 | all-reduce | flops 2048 | bytes 16384 | tf_op jit(solution)/shard_map/psum | solution.py:18
  162.5 8.8 %all-reduce.1 = (f32[1024]{0:T(1024)S(1)}, f32[1024]{0:T(1024)S(1)}) all-reduce(f32[1024]{0:T(1024)S(1)} %get-tuple-element.13, f32[1024]{0:T(1024)S(1)} %get-tuple-element.14), channel_id=1, replica_groups=mesh['hst_0'=4,'hst_1'=2,'dev_0'=4,'dev_1'=4] {'dev_0'}, use_global_device_ids=true, to_apply=%region_8.9 | all-reduce | flops 2048 | bytes 16384 | tf_op jit(solution)/shard_map/psum | solution.py:18
  171.4 9.4 %all-reduce = (f32[1024]{0:T(1024)S(1)}, f32[1024]{0:T(1024)S(1)}) all-reduce(f32[1024]{0:T(1024)S(1)} %get-tuple-element.9, f32[1024]{0:T(1024)S(1)} %get-tuple-element.10), channel_id=1, replica_groups=mesh['hst_0'=4,'hst_1'=2,'dev_0'=4,'dev_1'=4] {'dev_1'}, use_global_device_ids=true, to_apply=%region_9.10 | all-reduce | flops 2048 | bytes 16384 | tf_op jit(solution)/shard_map/psum | solution.py:18
  180.8 0.0 copy-done.9
  180.8 0.0 copy-done.10
  180.8 6.9 %maximum_convert_fusion = bf16[2048,1024]{1,0:T(8,128)(2,1)} fusion(f32[2048,1024]{1,0:T(8,128)} %get-tuple-element.47, f32[1024]{0:T(1024)S(1)} %copy-done.9, f32[1024]{0:T(1024)S(1)} %copy-done.10, f32[1024]{0:T(1024)S(1)} %get-tuple-element.46, f32[1024]{0:T(1024)S(1)} %get-tuple-element.45), kind=kLoop, calls=%fused_computation.21 | loop fusion | flops 12582912 | bytes 12599296 | tf_op jit(solution)/shard_map/convert_element_type | solution.py:69
  187.8 0.0 copy-start.6
  187.8 5.5 %gather_fusion.3 = bf16[512,1024]{1,0:T(8,128)(2,1)S(1)} fusion(bf16[2048,1024]{1,0:T(8,128)(2,1)} %maximum_convert_fusion, s32[1024]{0:T(1024)S(1)} %pad_clamp_fusion), kind=kCustom, calls=%fused_computation.3 | custom fusion | bytes 2099200 | tf_op jit(solution)/shard_map/jit(_take)/gather | solution.py:70
  193.2 1.2 broadcast_select_fusion.1
  194.4 3.7 %all-to-all-start.1 = ((bf16[16,32,1024]{2,1,0:T(8,128)(2,1)}), bf16[16,32,1024]{2,1,0:T(8,128)(2,1)S(1)}, u32[]{:S(2)}, u32[]{:S(2)}) async-start(bf16[16,32,1024]{2,1,0:T(8,128)(2,1)} %broadcast_select_fusion.1), calls=%async_computation.1 | async-start | bytes 2097152 | tf_op jit(solution)/shard_map/all_to_all | solution.py:71
  198.1 0.0 copy-done.6
  198.1 14.2 %all-to-all-done.1 = bf16[16,32,1024]{2,1,0:T(8,128)(2,1)S(1)} async-done(((bf16[16,32,1024]{2,1,0:T(8,128)(2,1)}), bf16[16,32,1024]{2,1,0:T(8,128)(2,1)S(1)}, u32[]{:S(2)}, u32[]{:S(2)}) %all-to-all-start.1) | async-done | bytes 1048608 | tf_op jit(solution)/shard_map/all_to_all | solution.py:71
  212.3 0.0 copy-start.1
  212.3 14.3 %fusion.39 = f32[512,153]{0,1:T(8,128)S(1)} fusion(bf16[1024,153]{0,1:T(8,128)(2,1)} %param.31, bf16[512,1024]{1,0:T(8,128)(2,1)S(1)} %bitcast.46, bf16[2048,1024]{1,0:T(8,128)(2,1)} %maximum_convert_fusion, s32[512]{0:T(512)S(1)} %bitcast.77, s32[512]{0:T(512)S(1)} %bitcast.78, s32[512]{0:T(512)S(1)} %bitcast.65, s32[512]{0:T(512)S(1)} %bitcast.66, ...), kind=kOutput, calls=%fused_computation.79 | convolution fusion | flops 2915303424 | bytes 5900288 | tf_op jit(solution)/shard_map/dot_general | solution.py:75
  226.6 0.0 copy-done.1
  226.6 2.5 %convolution_add_fusion.1 = f32[512,153]{0,1:T(8,128)} fusion(f32[512,153]{0,1:T(8,128)S(1)} %fusion.39, bf16[1024,153]{0,1:T(8,128)(2,1)S(1)} %copy-done.1, bf16[2048,1024]{1,0:T(8,128)(2,1)} %maximum_convert_fusion), kind=kOutput, calls=%fused_computation.80 | convolution fusion | flops 160510464 | bytes 1988608 | tf_op jit(solution)/shard_map/dot_general | solution.py:75
  (11 shorter events, 0.1 us)
Async XLA Ops:
  0.0 90.4 %copy-start = (bf16[768,1024]{1,0:T(8,128)(2,1)S(1)}, bf16[768,1024]{1,0:T(8,128)(2,1)}, u32[]{:S(2)}) copy-start(bf16[768,1024]{1,0:T(8,128)(2,1)} %param.27) | copy-start | bytes 4718596
  14.6 15.0 %copy-start.8 = (s32[1,512]{1,0:T(1,128)S(1)}, s32[1,512]{1,0:T(1,128)}, u32[]{:S(2)}) copy-start(s32[1,512]{1,0:T(1,128)} %param.25) | copy-start | bytes 6148
  14.6 15.8 %copy-start.5 = (s32[2048]{0:T(1024)S(1)}, s32[2048]{0:T(1024)}, u32[]{:S(2)}) copy-start(s32[2048]{0:T(1024)} %param.19) | copy-start | bytes 24580
  17.9 51.7 %all-to-all-start = ((bf16[128,16,768]{2,1,0:T(8,128)(2,1)}), bf16[128,16,768]{2,1,0:T(8,128)(2,1)}, u32[]{:S(2)}, u32[]{:S(2)}) async-start(bf16[128,16,768]{2,1,0:T(8,128)(2,1)} %broadcast_select_fusion), calls=%async_computation | async-start | bytes 6291456 | tf_op jit(solution)/shard_map/all_to_all | solution.py:52
  30.3 13.8 %copy-start.7 = (s32[2048]{0:T(1024)S(1)}, s32[2048]{0:T(1024)}, u32[]{:S(2)}) copy-start(s32[2048]{0:T(1024)} %param.18) | copy-start | bytes 24580
  30.4 13.8 %copy-start.3 = (s32[2048]{0:T(1024)S(1)}, s32[2048]{0:T(1024)}, u32[]{:S(2)}) copy-start(s32[2048]{0:T(1024)} %param.21) | copy-start | bytes 24580
  30.4 13.8 %copy-start.4 = (s32[2048]{0:T(1024)S(1)}, s32[2048]{0:T(1024)}, u32[]{:S(2)}) copy-start(s32[2048]{0:T(1024)} %param.20) | copy-start | bytes 24580
  30.4 13.9 %copy-start.2 = (s32[2048,15]{0,1:T(8,128)S(1)}, s32[2048,15]{0,1:T(8,128)}, u32[]{:S(2)}) copy-start(s32[2048,15]{0,1:T(8,128)} %param.23) | copy-start | bytes 368644
  90.4 90.4 %copy-start.9 = (f32[1024]{0:T(1024)S(1)}, f32[1024]{0:T(1024)}, u32[]{:S(2)}) copy-start(f32[1024]{0:T(1024)} %param.29) | copy-start | bytes 12292
  90.4 90.4 %copy-start.10 = (f32[1024]{0:T(1024)S(1)}, f32[1024]{0:T(1024)}, u32[]{:S(2)}) copy-start(f32[1024]{0:T(1024)} %param.28) | copy-start | bytes 12292
  187.8 10.3 %copy-start.6 = (s32[512,15]{0,1:T(8,128)S(1)}, s32[512,15]{0,1:T(8,128)}, u32[]{:S(2)}) copy-start(s32[512,15]{0,1:T(8,128)} %param.24) | copy-start | bytes 92164
  194.4 17.9 %all-to-all-start.1 = ((bf16[16,32,1024]{2,1,0:T(8,128)(2,1)}), bf16[16,32,1024]{2,1,0:T(8,128)(2,1)S(1)}, u32[]{:S(2)}, u32[]{:S(2)}) async-start(bf16[16,32,1024]{2,1,0:T(8,128)(2,1)} %broadcast_select_fusion.1), calls=%async_computation.1 | async-start | bytes 2097152 | tf_op jit(solution)/shard_map/all_to_all | solution.py:71
  212.3 14.3 %copy-start.1 = (bf16[1024,153]{0,1:T(8,128)(2,1)S(1)}, bf16[1024,153]{0,1:T(8,128)(2,1)}, u32[]{:S(2)}) copy-start(bf16[1024,153]{0,1:T(8,128)(2,1)} %param.30) | copy-start | bytes 940036
where the time goes:
time: 229 us
  matrix products  85.3 us (37%)
  local copies, waits for them, and re-layouts  44.2 us (19%)
  waiting for transfers between devices  39.5 us (17%)
  blocking collectives  30.1 us (13%)
  starting transfers between devices  15.3 us (7%)
  other arithmetic  14.4 us (6%)
    dot_general x1, matrix products, local(): jnp.dot(first_mean, neigh_first, preferred_element_type=jnp.float32)  60.2 us
    psum x4, blocking collectives, one_axis_at_a_time(): return functools.reduce(lax.psum, axes, array)  30.1 us
    all_to_all x1, waiting for transfers between devices, local(): lax.all_to_all(outgoing, HST_DEV, split_axis=0, concat_axis=0, tiled=True)  25.2 us
    dot_general x1, matrix products, local(): jnp.dot(second_mean, neigh_second, preferred_element_type=jnp.float32)  14.3 us
    all_to_all x1, waiting for transfers between devices, local(): lax.all_to_all(boundary, DEV, split_axis=0, concat_axis=0, tiled=True)  14.2 us
    gather x1, local copies, waits for them, and re-layouts, local(): hot_feat = jnp.take(hot_rows, hot_id, axis=0)  13.7 us
    gather x1, local copies, waits for them, and re-layouts, local(): cold_feat = jnp.take(arrived, cold_owner * slots + cold_pos, axis=0)  12.4 us
    gather x1, local copies, waits for them, and re-layouts, local(): outgoing = jnp.take(cold_rows, cold_send[0], axis=0)  11.7 us
  transfers between devices with their start and end apart: 2, of which 2 were waited for; matrix products, arithmetic and copies ran while one was open for 6% of the time, Pallas kernels for 0%

commit v1 on v0

v1 whole, which is shorter than its diff:
```python
import functools

import jax
import jax.numpy as jnp
from jax import lax
from jax.experimental import pallas as pl
from jax.experimental.pallas import tpu as pltpu
from jax.sharding import Mesh
from jax.sharding import PartitionSpec as P

HST = ("hst_0", "hst_1")
DEV = ("dev_0", "dev_1")
HST_DEV = ("hst_0", "hst_1", "dev_0", "dev_1")

LANES = 128
BLOCK = 512
epsilon = 1e-05

f32 = jnp.float32
bf16 = jnp.bfloat16


def row_to_lanes(row):
    return jnp.transpose(jnp.broadcast_to(row, (LANES, row.shape[1])))


def one_hot(row, width):
    spread = row_to_lanes(row).astype(jnp.int16)
    lane = lax.broadcasted_iota(jnp.int32, spread.shape, 1).astype(jnp.int16)
    one, zero = jnp.array(1, bf16), jnp.array(0, bf16)
    tiles = [
        jnp.where(spread == lane + jnp.int16(LANES * j), one, zero) for j in range(width // LANES)
    ]
    return jnp.concatenate(tiles, axis=1)


def params(**kw):
    return pltpu.CompilerParams(dimension_semantics=("arbitrary",), vmem_limit_bytes=60 * 2**20, **kw)


def whole(shape):
    return pl.BlockSpec(shape, lambda i: (0,) * len(shape))


def select_rows_kernel(idx_ref, table_ref, out_ref):
    hot = one_hot(idx_ref[...], table_ref.shape[0])
    out_ref[...] = jnp.dot(hot, table_ref[...], preferred_element_type=f32).astype(bf16)


def select_rows(idx, table):
    rows, width = idx.shape[1], table.shape[1]
    return pl.pallas_call(
        select_rows_kernel,
        grid=(rows // BLOCK,),
        in_specs=[pl.BlockSpec((1, BLOCK), lambda i: (0, i)), whole(table.shape)],
        out_specs=pl.BlockSpec((BLOCK, width), lambda i: (i, 0)),
        out_shape=jax.ShapeDtypeStruct((rows, width), bf16),
        compiler_params=params(),
        name="select_rows",
    )(idx, table)


def counts_kernel(adj_ref, out_ref):
    step = 16
    fanout = adj_ref.shape[1]
    width = out_ref.shape[1]
    lane = lax.broadcasted_iota(jnp.int32, (step, LANES), 1).astype(jnp.int16)
    one, zero = jnp.array(1, bf16), jnp.array(0, bf16)

    def body(r, carry):
        start = pl.multiple_of(r * step, step)
        rows = adj_ref[pl.ds(start, step), :]
        spread = [
            jnp.broadcast_to(rows[:, k : k + 1], (step, LANES)).astype(jnp.int16) for k in range(fanout)
        ]
        for j in range(width // LANES):
            here = lane + jnp.int16(LANES * j)
            acc = jnp.where(spread[0] == here, one, zero)
            for k in range(1, fanout):
                acc = acc + jnp.where(spread[k] == here, one, zero)
            out_ref[pl.ds(start, step), LANES * j : LANES * (j + 1)] = acc
        return carry

    lax.fori_loop(0, adj_ref.shape[0] // step, body, 0)


def counts(adjacency, width):
    rows, fanout = adjacency.shape
    block = min(rows, BLOCK)
    return pl.pallas_call(
        counts_kernel,
        grid=(rows // block,),
        in_specs=[pl.BlockSpec((block, fanout), lambda i: (i, 0))],
        out_specs=pl.BlockSpec((block, width), lambda i: (i, 0)),
        out_shape=jax.ShapeDtypeStruct((rows, width), bf16),
        compiler_params=params(),
        cost_estimate=pl.CostEstimate(
            flops=3 * fanout * rows * width, bytes_accessed=2 * rows * width, transcendentals=0
        ),
        name="neighbour_counts",
    )(adjacency)


def first_layer_kernel(
    slot_ref, arrived_ref, hot_ref, adj_ref, ws_ref, wn_ref, pre_ref, stat_ref, feat, acc, *, fanout
):
    i = pl.program_id(0)
    blocks = pl.num_programs(0) // 2

    @pl.when(i < blocks)
    def _():
        slot = slot_ref[...]
        pick = one_hot(slot, arrived_ref.shape[0])
        cold = jnp.dot(pick, arrived_ref[...], preferred_element_type=f32).astype(bf16)
        is_hot = row_to_lanes(slot) < 0
        reps = hot_ref.shape[1] // LANES
        cold = jnp.concatenate(
            [
                jnp.where(
                    is_hot,
                    hot_ref[:, LANES * j : LANES * (j + 1)].astype(f32),
                    cold[:, LANES * j : LANES * (j + 1)].astype(f32),
                ).astype(bf16)
                for j in range(reps)
            ],
            axis=1,
        )
        feat[pl.ds(pl.multiple_of(i * BLOCK, BLOCK), BLOCK), :] = cold

    @pl.when(i >= blocks)
    def _():
        b = i - blocks
        total = jnp.dot(adj_ref[...], feat[...], preferred_element_type=f32)
        mean = (total * (1.0 / fanout)).astype(bf16)
        own = feat[pl.ds(pl.multiple_of(b * BLOCK, BLOCK), BLOCK), :]
        pre = jnp.dot(own, ws_ref[...], preferred_element_type=f32) + jnp.dot(
            mean, wn_ref[...], preferred_element_type=f32
        )
        pre_ref[...] = pre
        grouped = pre.reshape(BLOCK // 8, 8, pre.shape[1])
        sums = jnp.sum(grouped, axis=0)
        squares = jnp.sum(grouped * grouped, axis=0)

        @pl.when(b == 0)
        def _():
            acc[0:8, :] = sums
            acc[8:16, :] = squares

        @pl.when(b > 0)
        def _():
            acc[0:8, :] += sums
            acc[8:16, :] += squares

        @pl.when(b == blocks - 1)
        def _():
            stat_ref[0:1, :] = jnp.sum(acc[0:8, :], axis=0, keepdims=True)
            stat_ref[1:2, :] = jnp.sum(acc[8:16, :], axis=0, keepdims=True)


def first_layer(slot, arrived, hot, adj, ws, wn, fanout):
    rows, width = adj.shape[0], hot.shape[1]
    hidden = ws.shape[1]
    blocks = rows // BLOCK
    first = lambda i: jnp.minimum(i, blocks - 1)
    second = lambda i: jnp.maximum(i - blocks, 0)
    return pl.pallas_call(
        functools.partial(first_layer_kernel, fanout=fanout),
        grid=(2 * blocks,),
        in_specs=[
            pl.BlockSpec((1, BLOCK), lambda i: (0, first(i))),
            whole(arrived.shape),
            pl.BlockSpec((BLOCK, width), lambda i: (first(i), 0)),
            pl.BlockSpec((BLOCK, rows), lambda i: (second(i), 0)),
            whole(ws.shape),
            whole(wn.shape),
        ],
        out_specs=[
            pl.BlockSpec((BLOCK, hidden), lambda i: (second(i), 0)),
            whole((2, hidden)),
        ],
        out_shape=[
            jax.ShapeDtypeStruct((rows, hidden), f32),
            jax.ShapeDtypeStruct((2, hidden), f32),
        ],
        scratch_shapes=[pltpu.VMEM((rows, width), bf16), pltpu.VMEM((16, hidden), f32)],
        compiler_params=params(),
        name="first_layer",
    )(slot, arrived, hot, adj, ws, wn)


def second_layer_kernel(
    pre_ref, stat_ref, gain_ref, shift_ref, send_ref, ws_ref, wn_ref, own_ref, neigh_ref, halo_ref, *, total_rows
):
    i = pl.program_id(0)
    mean = stat_ref[0:1, :] * (1.0 / total_rows)
    variance = stat_ref[1:2, :] * (1.0 / total_rows) - mean * mean
    scale = lax.rsqrt(variance + epsilon) * gain_ref[...]
    hidden = jnp.maximum((pre_ref[...] - mean) * scale + shift_ref[...], 0.0).astype(bf16)
    neigh = jnp.dot(hidden, wn_ref[...], preferred_element_type=f32).astype(bf16)
    neigh_ref[pl.ds(pl.multiple_of(i * BLOCK, BLOCK), BLOCK), :] = neigh

    @pl.when(i == 0)
    def _():
        own_ref[...] = jnp.dot(hidden, ws_ref[...], preferred_element_type=f32)

    @pl.when(i == pl.num_programs(0) - 1)
    def _():
        pick = one_hot(send_ref[...], neigh_ref.shape[0])
        halo_ref[...] = jnp.dot(pick, neigh_ref[...], preferred_element_type=f32).astype(bf16)


def second_layer(pre, stat, gain, shift, send, ws, wn, total_rows):
    rows, hidden = pre.shape
    classes = ws.shape[1]
    halo = send.shape[1]
    return pl.pallas_call(
        functools.partial(second_layer_kernel, total_rows=total_rows),
        grid=(rows // BLOCK,),
        in_specs=[
            pl.BlockSpec((BLOCK, hidden), lambda i: (i, 0)),
            whole((2, hidden)),
            whole((1, hidden)),
            whole((1, hidden)),
            whole((1, halo)),
            whole(ws.shape),
            whole(wn.shape),
        ],
        out_specs=[
            whole((BLOCK, classes)),
            whole((rows, classes)),
            whole((halo, classes)),
        ],
        out_shape=[
            jax.ShapeDtypeStruct((BLOCK, classes), f32),
            jax.ShapeDtypeStruct((rows, classes), bf16),
            jax.ShapeDtypeStruct((halo, classes), bf16),
        ],
        compiler_params=params(),
        name="second_layer",
    )(pre, stat, gain, shift, send, ws, wn)


def output_kernel(own_ref, adj_ref, neigh_ref, recv_ref, out_ref, *, fanout):
    rows = neigh_ref.shape[0]
    total = jnp.dot(adj_ref[:, :rows], neigh_ref[...], preferred_element_type=f32) + jnp.dot(
        adj_ref[:, rows:], recv_ref[...], preferred_element_type=f32
    )
    out_ref[...] = own_ref[...] + total * (1.0 / fanout)


def output(own, adj, neigh, recv, fanout):
    specs = [whole(a.shape) for a in (own, adj, neigh, recv)]
    return pl.pallas_call(
        functools.partial(output_kernel, fanout=fanout),
        grid=(1,),
        in_specs=specs,
        out_specs=whole(own.shape),
        out_shape=jax.ShapeDtypeStruct(own.shape, f32),
        compiler_params=params(),
        name="output_layer",
    )(own, adj, neigh, recv)


def local(
    hot_rows,
    cold_rows,
    hot_mask,
    hot_id,
    cold_owner,
    cold_pos,
    cold_send,
    adjacency_one,
    adjacency_two,
    halo_send,
    self_first,
    neigh_first,
    bn_gain,
    bn_shift,
    self_second,
    neigh_second,
):
    devices = lax.axis_size(HST_DEV)
    nodes = hot_mask.shape[0]
    targets = adjacency_two.shape[0]
    fan_one, fan_two = adjacency_one.shape[1], adjacency_two.shape[1]

    outgoing = select_rows(cold_send, cold_rows)
    slots = outgoing.shape[0] // devices
    arrived = lax.all_to_all(outgoing, HST_DEV, split_axis=0, concat_axis=0, tiled=True)

    hot_feat = hot_rows.at[hot_id].get(mode="promise_in_bounds")
    adj_one = counts(adjacency_one, nodes)
    adj_two = counts(adjacency_two, nodes + halo_send.shape[1])
    slot = jnp.where(hot_mask == 1, -1, cold_owner * slots + cold_pos)[None, :]

    pre, stat = first_layer(slot, arrived, hot_feat, adj_one, self_first, neigh_first, fan_one)
    stat = functools.reduce(lax.psum, HST_DEV, stat)
    own, neigh, halo = second_layer(
        pre,
        stat,
        bn_gain[None, :],
        bn_shift[None, :],
        halo_send,
        self_second,
        neigh_second,
        nodes * devices,
    )
    recv = lax.all_to_all(halo, DEV, split_axis=0, concat_axis=0, tiled=True)
    return output(own, adj_two, neigh, recv, fan_two)


def solution(mesh):
    torus = Mesh(mesh.devices.reshape(4, 2, 4, 4), ("hst_0", "hst_1", "dev_0", "dev_1"))
    split = P(HST_DEV)
    rows = P(HST_DEV, None)
    return jax.shard_map(
        local,
        mesh=torus,
        in_specs=(P(), rows, split, split, split, split, rows, rows, rows, rows, P(), P(), P(), P(), P(), P()),
        out_specs=rows,
        check_vma=False,
    )
```

time: 229 us -> 159 us (0.69)
  matrix products: 85.3 us -> 0 us
  Pallas kernels: 0 us -> 83.5 us
  waiting for transfers between devices: 39.5 us -> 0.01 us
  local copies, waits for them, and re-layouts: 44.2 us -> 24.1 us
  other arithmetic: 14.4 us -> 0.61 us
  blocking collectives: 30.1 us -> 35.1 us
    dot_general x4 -> x0, matrix products: 85.3 us -> none  [the longest x1 60.2 us: local(): jnp.dot(first_mean, neigh_first, preferred_element_type=jnp.float32)]
    pallas_call x0 -> x6, Pallas kernels: none -> 83.5 us  [the longest x2 33.3 us: counts(): pl.pallas_call(counts_kernel, grid=(rows // block,), in_specs=[pl.BlockSp...]
    gather x4 -> x1, local copies, waits for them, and re-layouts: 43.4 us -> 13.7 us  [local(): hot_feat = hot_rows.at[hot_id].get(mode='promise_in_bounds')]
    all_to_all x1, waiting for transfers between devices: 25.2 us -> 0.01 us  [local(): lax.all_to_all(outgoing, HST_DEV, split_axis=0, concat_axis=0, tiled=True)]
    all_to_all x1, waiting for transfers between devices: 14.2 us -> 0.01 us  [local(): recv = lax.all_to_all(halo, DEV, split_axis=0, concat_axis=0, tiled=True)]
    unnamed x23 -> x20, local copies, waits for them, and re-layouts: 0.56 us -> 8.49 us
    convert_element_type x1 -> x0, other arithmetic: 6.95 us -> none  [local(): hidden = jax.nn.relu((hidden_pre - mean) * lax.rsqrt(variance + epsilon)...]
    psum x4, blocking collectives: 30.1 us -> 35.1 us  [local(): stat = functools.reduce(lax.psum, HST_DEV, stat)]
  transfers between devices with their start and end apart: 2 -> 2, of which waited for: 2 -> 0; matrix products, arithmetic and copies ran while one was open for 6% -> 13% of each run, Pallas kernels for 0% -> 21%
where the time goes in v1:
time: 159 us; the launch traced here: 158 us
  Pallas kernels  83.5 us (53%)
  blocking collectives  35.1 us (22%)
  local copies, waits for them, and re-layouts  24.1 us (15%)
  starting transfers between devices  14.7 us (9%)
    psum x4, blocking collectives, local(): stat = functools.reduce(lax.psum, HST_DEV, stat)  35.1 us
    pallas_call x2, Pallas kernels, counts(): pl.pallas_call(counts_kernel, grid=(rows // block,), in_specs=[pl.BlockSp...  33.3 us
    pallas_call x1, Pallas kernels, first_layer(): pl.pallas_call(functools.partial(first_layer_kernel, fanout=fanout), grid...  32.1 us
    gather x1, local copies, waits for them, and re-layouts, local(): hot_feat = hot_rows.at[hot_id].get(mode='promise_in_bounds')  13.7 us
    all_to_all x1, starting transfers between devices, local(): lax.all_to_all(outgoing, HST_DEV, split_axis=0, concat_axis=0, tiled=True)  11.2 us
    unnamed x20, local copies, waits for them, and re-layouts  8.49 us
    pallas_call x1, Pallas kernels, second_layer(): pl.pallas_call(functools.partial(second_layer_kernel, total_rows=total_ro...  7.68 us
    pallas_call x1, Pallas kernels, select_rows(): pl.pallas_call(select_rows_kernel, grid=(rows // BLOCK,), in_specs=[pl.Bl...  6.46 us
  transfers between devices with their start and end apart: 2, of which 0 were waited for; matrix products, arithmetic and copies ran while one was open for 13% of the time, Pallas kernels for 21%

profile of v1, /device:TPU:0, one launch (start us, length us, event | category | flops | bytes accessed | tf_op | source)
XLA Modules:
  0.0 158.1 jit_solution(12289004747819430897)
XLA Ops:
  0.0 6.5 %select_rows.1 = bf16[2048,768]{1,0:T(8,128)(2,1)} custom-call(s32[1,2048]{1,0:T(1,128)} %idx_ref.1, bf16[1024,768]{1,0:T(8,128)(2,1)} %table_ref.1), custom_call_target="tpu_custom_call" | custom-call | tf_op jit(solution)/shard_map/select_rows/pallas_call | solution.py:52
  6.5 0.0 copy-start.2
  6.5 0.0 copy-start.4
  6.5 11.2 %all-to-all-start = ((bf16[128,16,768]{2,1,0:T(8,128)(2,1)}), bf16[128,16,768]{2,1,0:T(8,128)(2,1)S(1)}, u32[]{:S(2)}, u32[]{:S(2)}) async-start(bf16[128,16,768]{2,1,0:T(8,128)(2,1)} %bitcast.7), calls=%async_computation | async-start | bytes 6291456 | tf_op jit(solution)/shard_map/all_to_all | solution.py:289
  17.6 2.2 %copy.17.adj_ref = s32[2048,15]{1,0:T(8,128)} copy(s32[2048,15]{0,1:T(8,128)} %param.23) | data formatting | bytes 245760 | tf_op args[7]
  19.9 0.0 copy-done.2
  19.9 1.0 copy.18.ws_ref
  20.9 2.0 %copy.19.wn_ref = bf16[1024,153]{1,0:T(8,128)(2,1)} copy(bf16[1024,153]{0,1:T(8,128)(2,1)} %param.31) | data formatting | bytes 626688 | tf_op args[15]
  22.9 0.0 copy-done.4
  22.9 13.7 %gather_fusion = bf16[2048,768]{1,0:T(8,128)(2,1)} fusion(bf16[4096,768]{1,0:T(8,128)(2,1)} %param.16, s32[2048]{0:T(1024)S(1)} %fusion), kind=kCustom, calls=%fused_computation | custom fusion | bytes 6299648 | tf_op jit(solution)/shard_map/gather | solution.py:291
  36.6 0.0 copy-start.5
  36.6 0.0 copy-start.6
  36.6 0.0 copy-start.7
  36.6 24.5 %neighbour_counts.2.adj_ref = bf16[2048,2048]{1,0:T(8,128)(2,1)} custom-call(s32[2048,15]{1,0:T(8,128)} %copy.17.adj_ref), custom_call_target="tpu_custom_call" | custom-call | flops 188743680 | bytes 8388608 | tf_op jit(solution)/shard_map/neighbour_counts/pallas_call | solution.py:90
  61.1 0.0 copy-done.5
  61.1 0.0 copy-done.6
  61.1 0.0 copy-done.7
  61.1 0.6 add_select_fusion
  61.8 0.0 all-to-all-done
  61.8 0.0 copy-start
  61.8 1.7 %copy-done = bf16[128,16,768]{2,1,0:T(8,128)(2,1)} copy-done((bf16[128,16,768]{2,1,0:T(8,128)(2,1)}, bf16[128,16,768]{2,1,0:T(8,128)(2,1)S(1)}, u32[]{:S(2)}) %copy-start) | copy-done | bytes 3145752
  63.4 32.1 %first_layer.1 = (f32[2048,1024]{1,0:T(8,128)}, f32[2,1024]{1,0:T(2,128)}) custom-call(s32[1,2048]{1,0:T(1,128)} %bitcast.11, bf16[2048,768]{1,0:T(8,128)(2,1)} %bitcast.8, bf16[2048,768]{1,0:T(8,128)(2,1)} %gather_fusion, bf16[2048,2048]{1,0:T(8,128)(2,1)} %neighbour_counts.2.adj_ref, bf16[768,1024]{1,0:T(8,128)(2,1)} %ws_ref.2, bf16[768,1024]{1,0:T(8,128)(2,1)} %wn_ref.2), custom_call_target="tpu_custom_call" | custom-call | tf_op jit(solution)/shard_map/first_layer/pallas_call | solution.py:166
  95.6 10.2 %psum.28 = f32[2,1024]{1,0:T(2,128)S(1)} all-reduce(f32[2,1024]{1,0:T(2,128)} %get-tuple-element.11), channel_id=1, replica_groups=mesh['hst_0'=4,'hst_1'=2,'dev_0'=4,'dev_1'=4] {'hst_0'}, use_global_device_ids=true, to_apply=%region_0.1 | all-reduce | flops 2048 | bytes 16384 | tf_op jit(solution)/shard_map/psum | solution.py:297
  105.8 2.5 %psum.29 = f32[2,1024]{1,0:T(2,128)S(1)} all-reduce(f32[2,1024]{1,0:T(2,128)S(1)} %psum.28), channel_id=1, replica_groups=mesh['hst_0'=4,'hst_1'=2,'dev_0'=4,'dev_1'=4] {'hst_1'}, use_global_device_ids=true, to_apply=%region_1.2 | all-reduce | flops 2048 | bytes 16384 | tf_op jit(solution)/shard_map/psum | solution.py:297
  108.3 11.3 %psum.30 = f32[2,1024]{1,0:T(2,128)S(1)} all-reduce(f32[2,1024]{1,0:T(2,128)S(1)} %psum.29), channel_id=1, replica_groups=mesh['hst_0'=4,'hst_1'=2,'dev_0'=4,'dev_1'=4] {'dev_0'}, use_global_device_ids=true, to_apply=%region_2.3 | all-reduce | flops 2048 | bytes 16384 | tf_op jit(solution)/shard_map/psum | solution.py:297
  119.6 11.1 %psum.31.stat_ref = f32[2,1024]{1,0:T(2,128)} all-reduce(f32[2,1024]{1,0:T(2,128)S(1)} %psum.30), channel_id=1, replica_groups=mesh['hst_0'=4,'hst_1'=2,'dev_0'=4,'dev_1'=4] {'dev_1'}, use_global_device_ids=true, to_apply=%region_3.4 | all-reduce | flops 2048 | bytes 16384 | tf_op jit(solution)/shard_map/psum | solution.py:297
  130.7 0.0 copy-start.3
  130.7 7.7 %second_layer.1 = (f32[512,153]{1,0:T(8,128)}, bf16[2048,153]{1,0:T(8,128)(2,1)}, bf16[512,153]{1,0:T(8,128)(2,1)}) custom-call(f32[2048,1024]{1,0:T(8,128)} %get-tuple-element.10.pre_ref, f32[2,1024]{1,0:T(2,128)} %psum.31.stat_ref, f32[1,1024]{1,0:T(1,128)} %bitcast.12, f32[1,1024]{1,0:T(1,128)} %bitcast.13, s32[1,512]{1,0:T(1,128)} %send_ref.1, ...), custom_call_target="tpu_custom_call" | custom-call | tf_op jit(solution)/shard_map/second_layer/pallas_call | solution.py:216
  138.4 3.5 %all-to-all-start.1 = ((bf16[16,32,153]{2,1,0:T(8,128)(2,1)}), bf16[16,32,153]{2,1,0:T(8,128)(2,1)S(1)}, u32[]{:S(2)}, u32[]{:S(2)}) async-start(bf16[16,32,153]{2,1,0:T(8,128)(2,1)} %bitcast.10), calls=%async_computation.1 | async-start | bytes 524288 | tf_op jit(solution)/shard_map/all_to_all | solution.py:308
  141.9 0.0 copy-done.3
  141.9 0.9 copy.20.adj_ref
  142.8 8.8 %neighbour_counts.3.adj_ref = bf16[512,2560]{1,0:T(8,128)(2,1)} custom-call(s32[512,15]{1,0:T(8,128)} %copy.20.adj_ref), custom_call_target="tpu_custom_call" | custom-call | flops 58982400 | bytes 2621440 | tf_op jit(solution)/shard_map/neighbour_counts/pallas_call | solution.py:90
  151.6 0.0 all-to-all-done.1
  151.6 0.0 copy-start.1
  151.6 0.7 copy-done.1
  152.3 3.9 %output_layer.1 = f32[512,153]{1,0:T(8,128)} custom-call(f32[512,153]{1,0:T(8,128)} %get-tuple-element.12.own_ref, bf16[512,2560]{1,0:T(8,128)(2,1)} %neighbour_counts.3.adj_ref, bf16[2048,153]{1,0:T(8,128)(2,1)} %get-tuple-element.13.neigh_ref, bf16[512,153]{1,0:T(8,128)(2,1)} %bitcast.9), custom_call_target="tpu_custom_call" | custom-call | tf_op jit(solution)/shard_map/output_layer/pallas_call | solution.py:253
  156.2 1.9 %copy.21 = f32[512,153]{0,1:T(8,128)} copy(f32[512,153]{1,0:T(8,128)} %output_layer.1) | data formatting | bytes 626688 | tf_op jit(solution)/shard_map/output_layer/pallas_call | solution.py:253
  (1 shorter events, 0.0 us)
Async XLA Ops:
  6.5 13.4 %copy-start.2 = (bf16[1024,153]{0,1:T(8,128)(2,1)S(1)}, bf16[1024,153]{0,1:T(8,128)(2,1)}, u32[]{:S(2)}) copy-start(bf16[1024,153]{0,1:T(8,128)(2,1)} %param.30) | copy-start | bytes 940036
  6.5 16.4 %copy-start.4 = (s32[2048]{0:T(1024)S(1)}, s32[2048]{0:T(1024)}, u32[]{:S(2)}) copy-start(s32[2048]{0:T(1024)} %param.19) | copy-start | bytes 24580
  6.5 55.3 %all-to-all-start = ((bf16[128,16,768]{2,1,0:T(8,128)(2,1)}), bf16[128,16,768]{2,1,0:T(8,128)(2,1)S(1)}, u32[]{:S(2)}, u32[]{:S(2)}) async-start(bf16[128,16,768]{2,1,0:T(8,128)(2,1)} %bitcast.7), calls=%async_computation | async-start | bytes 6291456 | tf_op jit(solution)/shard_map/all_to_all | solution.py:289
  36.6 24.5 %copy-start.5 = (s32[2048]{0:T(1024)S(1)}, s32[2048]{0:T(1024)}, u32[]{:S(2)}) copy-start(s32[2048]{0:T(1024)} %param.21) | copy-start | bytes 24580
  36.6 24.5 %copy-start.6 = (s32[2048]{0:T(1024)S(1)}, s32[2048]{0:T(1024)}, u32[]{:S(2)}) copy-start(s32[2048]{0:T(1024)} %param.20) | copy-start | bytes 24580
  36.6 24.5 %copy-start.7 = (s32[2048]{0:T(1024)S(1)}, s32[2048]{0:T(1024)}, u32[]{:S(2)}) copy-start(s32[2048]{0:T(1024)} %param.18) | copy-start | bytes 24580
  61.8 1.7 %copy-start = (bf16[128,16,768]{2,1,0:T(8,128)(2,1)}, bf16[128,16,768]{2,1,0:T(8,128)(2,1)S(1)}, u32[]{:S(2)}) copy-start(bf16[128,16,768]{2,1,0:T(8,128)(2,1)S(1)} %all-to-all-done) | copy-start | bytes 9437188
  130.7 11.2 %copy-start.3 = (s32[512,15]{0,1:T(8,128)S(1)}, s32[512,15]{0,1:T(8,128)}, u32[]{:S(2)}) copy-start(s32[512,15]{0,1:T(8,128)} %param.24) | copy-start | bytes 92164
  138.4 13.2 %all-to-all-start.1 = ((bf16[16,32,153]{2,1,0:T(8,128)(2,1)}), bf16[16,32,153]{2,1,0:T(8,128)(2,1)S(1)}, u32[]{:S(2)}, u32[]{:S(2)}) async-start(bf16[16,32,153]{2,1,0:T(8,128)(2,1)} %bitcast.10), calls=%async_computation.1 | async-start | bytes 524288 | tf_op jit(solution)/shard_map/all_to_all | solution.py:308
  151.6 0.7 copy-start.1

commit v2 on v1

v2 whole, which is shorter than its diff:
```python
import functools

import jax
import jax.numpy as jnp
from jax import lax
from jax.experimental import pallas as pl
from jax.experimental.pallas import tpu as pltpu
from jax.sharding import Mesh
from jax.sharding import PartitionSpec as P

HST = ("hst_0", "hst_1")
DEV = ("dev_0", "dev_1")
HST_DEV = ("hst_0", "hst_1", "dev_0", "dev_1")

LANES = 128
BLOCK = 512
epsilon = 1e-05

f32 = jnp.float32
bf16 = jnp.bfloat16


def row_to_lanes(row):
    return jnp.transpose(jnp.broadcast_to(row, (LANES, row.shape[1])))


def one_hot(row, width):
    spread = row_to_lanes(row).astype(jnp.int16)
    lane = lax.broadcasted_iota(jnp.int32, spread.shape, 1).astype(jnp.int16)
    one, zero = jnp.array(1, bf16), jnp.array(0, bf16)
    tiles = [
        jnp.where(spread == lane + jnp.int16(LANES * j), one, zero) for j in range(width // LANES)
    ]
    return jnp.concatenate(tiles, axis=1)


VM = pl.BlockSpec(memory_space=pltpu.VMEM)
HBM = pl.BlockSpec(memory_space=pl.ANY)


def resident(array):
    return pltpu.with_memory_space_constraint(array, pltpu.VMEM)


def in_hbm(array):
    return pltpu.with_memory_space_constraint(array, pltpu.HBM)


def params(mib):
    return pltpu.CompilerParams(vmem_limit_bytes=mib * 2**20)


def whole(shape):
    return pl.BlockSpec(shape, lambda i: (0,) * len(shape))


def select_rows_kernel(idx_ref, table_ref, out_ref):
    hot = one_hot(idx_ref[...], table_ref.shape[0])
    out_ref[...] = jnp.dot(hot, table_ref[...], preferred_element_type=f32).astype(bf16)


def select_rows(idx, table):
    rows, width = idx.shape[1], table.shape[1]
    return pl.pallas_call(
        select_rows_kernel,
        grid=(rows // BLOCK,),
        in_specs=[pl.BlockSpec((1, BLOCK), lambda i: (0, i)), whole(table.shape)],
        out_specs=pl.BlockSpec((BLOCK, width), lambda i: (i, 0)),
        out_shape=pltpu.HBM((rows, width), bf16),
        compiler_params=params(24),
        name="select_rows",
    )(in_hbm(idx), in_hbm(table))


def count_neighbours(adj_ref, out_ref):
    step = 16
    group = 4
    fanout = adj_ref.shape[1]
    width = out_ref.shape[1]
    lane = lax.broadcasted_iota(jnp.int32, (step, LANES), 1).astype(jnp.int16)
    one, zero = jnp.array(1, bf16), jnp.array(0, bf16)

    def body(r, carry):
        for g in range(group):
            start = pl.multiple_of((r * group + g) * step, step)
            rows = adj_ref[pl.ds(start, step), :]
            spread = [
                jnp.broadcast_to(rows[:, k : k + 1], (step, LANES)).astype(jnp.int16) for k in range(fanout)
            ]
            for j in range(width // LANES):
                here = lane + jnp.int16(LANES * j)
                acc = jnp.where(spread[0] == here, one, zero)
                for k in range(1, fanout):
                    acc = acc + jnp.where(spread[k] == here, one, zero)
                out_ref[pl.ds(start, step), LANES * j : LANES * (j + 1)] = acc
        return carry

    lax.fori_loop(0, adj_ref.shape[0] // (step * group), body, 0)


def counts(adjacency, width):
    rows, fanout = adjacency.shape
    block = BLOCK // 2
    return pl.pallas_call(
        count_neighbours,
        grid=(rows // block,),
        in_specs=[pl.BlockSpec((block, fanout), lambda i: (i, 0))],
        out_specs=pl.BlockSpec((block, width), lambda i: (i, 0)),
        out_shape=pltpu.HBM((rows, width), bf16),
        compiler_params=params(24),
        cost_estimate=pl.CostEstimate(
            flops=3 * fanout * rows * width, bytes_accessed=2 * rows * width, transcendentals=0
        ),
        name="neighbour_counts",
    )(in_hbm(adjacency))


def first_layer_kernel(
    slot_ref, arrived_ref, hot_hbm, adj_hbm, ws_hbm, wn_hbm, pre_hbm, stat_ref,
    hot_ref, adj_ref, w_ref, pre_ref, hot_sem, adj_sem, ws_sem, wn_sem, pre_sem, both_ref, *, fanout
):
    rows, width = hot_ref.shape
    blocks = rows // BLOCK
    at = [pl.ds(b * BLOCK, BLOCK) for b in range(blocks)]
    hot_in = [pltpu.make_async_copy(hot_hbm.at[at[b]], hot_ref.at[at[b]], hot_sem.at[b]) for b in range(blocks)]
    adj_in = [pltpu.make_async_copy(adj_hbm.at[at[b]], adj_ref.at[at[b]], adj_sem.at[b]) for b in range(blocks)]
    ws_in = pltpu.make_async_copy(ws_hbm, w_ref.at[pl.ds(0, width)], ws_sem)
    wn_in = pltpu.make_async_copy(wn_hbm, w_ref.at[pl.ds(width, width)], wn_sem)
    pre_out = [pltpu.make_async_copy(pre_ref.at[b], pre_hbm.at[at[b]], pre_sem.at[b]) for b in range(blocks)]
    for copy in hot_in + [ws_in, wn_in] + adj_in:
        copy.start()
    for b in range(blocks):
        slot = slot_ref[:, at[b]]
        cold = jnp.dot(one_hot(slot, arrived_ref.shape[0]), arrived_ref[...], preferred_element_type=f32)
        is_hot = row_to_lanes(slot) < 0
        hot_in[b].wait()
        for j in range(width // LANES):
            lanes = slice(LANES * j, LANES * (j + 1))
            both_ref[at[b], lanes] = jnp.where(is_hot, hot_ref[at[b], lanes].astype(f32), cold[:, lanes]).astype(bf16)
    for b in range(blocks):
        adj_in[b].wait()
        total = jnp.dot(adj_ref[at[b], :], both_ref[:, :width], preferred_element_type=f32)
        both_ref[at[b], width:] = (total * (1.0 / fanout)).astype(bf16)
    ws_in.wait()
    wn_in.wait()
    sums = squares = 0
    for b in range(blocks):
        pre = jnp.dot(both_ref[at[b], :], w_ref[...], preferred_element_type=f32)
        pre_ref[b] = pre
        pre_out[b].start()
        grouped = pre.reshape(BLOCK // 8, 8, pre.shape[1])
        sums = sums + jnp.sum(grouped, axis=0)
        squares = squares + jnp.sum(grouped * grouped, axis=0)
    stat_ref[0:1, :] = jnp.sum(sums, axis=0, keepdims=True)
    stat_ref[1:2, :] = jnp.sum(squares, axis=0, keepdims=True)
    for b in range(blocks):
        pre_out[b].wait()


def first_layer(slot, arrived, hot, adj, ws, wn, fanout):
    rows, width = hot.shape
    hidden = ws.shape[1]
    blocks = rows // BLOCK
    return pl.pallas_call(
        functools.partial(first_layer_kernel, fanout=fanout),
        in_specs=[VM, VM, HBM, HBM, HBM, HBM],
        out_specs=[HBM, VM],
        out_shape=[
            pltpu.HBM((rows, hidden), f32),
            jax.ShapeDtypeStruct((2, hidden), f32),
        ],
        scratch_shapes=[
            pltpu.VMEM(hot.shape, bf16),
            pltpu.VMEM((rows, rows), bf16),
            pltpu.VMEM((2 * width, hidden), bf16),
            pltpu.VMEM((blocks, BLOCK, hidden), f32),
            pltpu.SemaphoreType.DMA((blocks,)),
            pltpu.SemaphoreType.DMA((blocks,)),
            pltpu.SemaphoreType.DMA,
            pltpu.SemaphoreType.DMA,
            pltpu.SemaphoreType.DMA((blocks,)),
            pltpu.VMEM((rows, 2 * width), bf16),
        ],
        compiler_params=params(48),
        name="first_layer",
    )(slot, resident(arrived), in_hbm(hot), in_hbm(adj), in_hbm(ws), in_hbm(wn))


def nt_dot(a, b):
    return lax.dot_general(a, b, (((1,), (1,)), ((), ())), preferred_element_type=f32)


def second_layer_kernel(
    pre_hbm, stat_ref, gain_ref, shift_ref, send_ref, ws_hbm, wn_hbm, own_hbm, neigh_hbm, halo_ref,
    pre_ref, ws_ref, wn_ref, own_ref, neigh_ref, pre_sem, ws_sem, wn_sem, own_sem, neigh_sem, *, total_rows
):
    blocks = pre_ref.shape[0] // BLOCK
    at = [pl.ds(b * BLOCK, BLOCK) for b in range(blocks)]
    pre_in = [pltpu.make_async_copy(pre_hbm.at[at[b]], pre_ref.at[at[b]], pre_sem.at[b]) for b in range(blocks)]
    ws_in = pltpu.make_async_copy(ws_hbm, ws_ref, ws_sem)
    wn_in = pltpu.make_async_copy(wn_hbm, wn_ref, wn_sem)
    own_out = pltpu.make_async_copy(own_ref, own_hbm, own_sem)
    neigh_out = pltpu.make_async_copy(neigh_ref, neigh_hbm, neigh_sem)
    for copy in [pre_in[0], wn_in, ws_in] + pre_in[1:]:
        copy.start()
    mean = stat_ref[0:1, :] * (1.0 / total_rows)
    variance = stat_ref[1:2, :] * (1.0 / total_rows) - mean * mean
    scale = lax.rsqrt(variance + epsilon) * gain_ref[...]
    shift = shift_ref[...]
    for b in range(blocks):
        pre_in[b].wait()
        hidden = jnp.maximum((pre_ref[at[b], :] - mean) * scale + shift, 0.0).astype(bf16)
        if b == 0:
            wn_in.wait()
            ws_in.wait()
            own_ref[...] = nt_dot(hidden, ws_ref[...])
            own_out.start()
        neigh_ref[at[b], :] = nt_dot(hidden, wn_ref[...]).astype(bf16)
    neigh_out.start()
    pick = one_hot(send_ref[...], neigh_ref.shape[0])
    halo_ref[...] = jnp.dot(pick, neigh_ref[...], preferred_element_type=f32).astype(bf16)
    own_out.wait()
    neigh_out.wait()


def second_layer(pre, stat, gain, shift, send, ws, wn, total_rows):
    rows, hidden = pre.shape
    classes = ws.shape[0]
    halo = send.shape[1]
    dma = pltpu.SemaphoreType.DMA
    return pl.pallas_call(
        functools.partial(second_layer_kernel, total_rows=total_rows),
        in_specs=[HBM, VM, VM, VM, VM, HBM, HBM],
        out_specs=[HBM, HBM, VM],
        out_shape=[
            pltpu.HBM((BLOCK, classes), f32),
            pltpu.HBM((rows, classes), bf16),
            jax.ShapeDtypeStruct((halo, classes), bf16),
        ],
        scratch_shapes=[
            pltpu.VMEM(pre.shape, f32),
            pltpu.VMEM(ws.shape, bf16),
            pltpu.VMEM(wn.shape, bf16),
            pltpu.VMEM((BLOCK, classes), f32),
            pltpu.VMEM((rows, classes), bf16),
            dma((rows // BLOCK,)),
            dma,
            dma,
            dma,
            dma,
        ],
        compiler_params=params(32),
        name="second_layer",
    )(in_hbm(pre), stat, gain, shift, send, in_hbm(ws), in_hbm(wn))


def targets_kernel(adj_ref, own_hbm, neigh_hbm, part_ref, far_ref, count_ref, own_ref, neigh_ref, own_sem, neigh_sem):
    rows = neigh_ref.shape[0]
    own_in = pltpu.make_async_copy(own_hbm, own_ref, own_sem)
    neigh_in = pltpu.make_async_copy(neigh_hbm, neigh_ref, neigh_sem)
    own_in.start()
    neigh_in.start()
    count_neighbours(adj_ref, count_ref)
    own_in.wait()
    neigh_in.wait()
    total = jnp.dot(count_ref[:, :rows], neigh_ref[...], preferred_element_type=f32)
    part_ref[...] = own_ref[...] + total * (1.0 / adj_ref.shape[1])
    far_ref[...] = count_ref[:, rows:]


def targets_layer(adj, own, neigh, halo):
    count, rows = adj.shape[0], neigh.shape[0]
    return pl.pallas_call(
        targets_kernel,
        in_specs=[VM, HBM, HBM],
        out_specs=[VM, VM],
        out_shape=[jax.ShapeDtypeStruct(own.shape, f32), jax.ShapeDtypeStruct((count, halo), bf16)],
        scratch_shapes=[
            pltpu.VMEM((count, rows + halo), bf16),
            pltpu.VMEM(own.shape, f32),
            pltpu.VMEM(neigh.shape, bf16),
            pltpu.SemaphoreType.DMA,
            pltpu.SemaphoreType.DMA,
        ],
        compiler_params=params(16),
        cost_estimate=pl.CostEstimate(
            flops=3 * adj.shape[1] * count * (rows + halo), bytes_accessed=2 * count * rows, transcendentals=0
        ),
        name="targets_layer",
    )(adj, in_hbm(own), in_hbm(neigh))


def output_kernel(part_ref, far_ref, recv_ref, out_ref, *, fanout):
    total = jnp.dot(far_ref[...], recv_ref[...], preferred_element_type=f32)
    out_ref[...] = jnp.transpose(part_ref[...] + total * (1.0 / fanout))


def output(part, far, recv, fanout):
    return pl.pallas_call(
        functools.partial(output_kernel, fanout=fanout),
        in_specs=[VM] * 3,
        out_specs=VM,
        out_shape=jax.ShapeDtypeStruct(part.shape[::-1], f32),
        compiler_params=params(16),
        name="output_layer",
    )(part, far, recv).T


def sum_over(array, axes):
    copies = jnp.broadcast_to(array[None], (lax.axis_size(axes),) + array.shape)
    return jnp.sum(lax.all_to_all(copies, axes, split_axis=0, concat_axis=0, tiled=True), axis=0)


def local(
    hot_rows,
    cold_rows,
    hot_mask,
    hot_id,
    cold_owner,
    cold_pos,
    cold_send,
    adjacency_one,
    adjacency_two,
    halo_send,
    self_first,
    neigh_first,
    bn_gain,
    bn_shift,
    self_second,
    neigh_second,
):
    devices = lax.axis_size(HST_DEV)
    nodes = hot_mask.shape[0]
    fan_one, fan_two = adjacency_one.shape[1], adjacency_two.shape[1]

    outgoing = select_rows(cold_send, cold_rows)
    slots = outgoing.shape[0] // devices
    arrived = lax.all_to_all(outgoing, HST_DEV, split_axis=0, concat_axis=0, tiled=True)

    hot_feat = hot_rows.at[hot_id].get(mode="promise_in_bounds")
    adj_one = counts(adjacency_one, nodes)
    slot = jnp.where(hot_mask == 1, -1, cold_owner * slots + cold_pos)[None, :]

    pre, stat = first_layer(slot, arrived, hot_feat, adj_one, self_first, neigh_first, fan_one)
    stat = sum_over(sum_over(stat, HST), DEV)
    own, neigh, halo = second_layer(
        pre,
        stat,
        bn_gain[None, :],
        bn_shift[None, :],
        halo_send,
        self_second.T,
        neigh_second.T,
        nodes * devices,
    )
    recv = lax.all_to_all(halo, DEV, split_axis=0, concat_axis=0, tiled=True)
    part, far = targets_layer(adjacency_two, own, neigh, halo_send.shape[1])
    return output(part, far, recv, fan_two)


def solution(mesh):
    torus = Mesh(mesh.devices.reshape(4, 2, 4, 4), ("hst_0", "hst_1", "dev_0", "dev_1"))
    split = P(HST_DEV)
    rows = P(HST_DEV, None)
    return jax.shard_map(
        local,
        mesh=torus,
        in_specs=(P(), rows, split, split, split, split, rows, rows, rows, rows, P(), P(), P(), P(), P(), P()),
        out_specs=rows,
        check_vma=False,
    )
```

time: 159 us -> 128 us (0.81)
  Pallas kernels: 83.5 us -> 66.4 us
  blocking collectives: 35.1 us -> 19.9 us
  waiting for transfers between devices: 0.01 us -> 10.9 us
  local copies, waits for them, and re-layouts: 24.1 us -> 15.3 us
    psum x4 -> x0, blocking collectives: 35.1 us -> none  [local(): stat = functools.reduce(lax.psum, HST_DEV, stat)]
    all_to_all x0 -> x2, blocking collectives: none -> 19.9 us  [sum_over(): lax.all_to_all(copies, axes, split_axis=0, concat_axis=0, tiled=True)]
    pallas_call x4, Pallas kernels: 69.3 us -> 52.2 us  [the longest x1 28.2 us: first_layer(): pl.pallas_call(functools.partial(first_layer_kernel, fanout=fanout), in_s...]
    all_to_all x1, waiting for transfers between devices: 0.01 us -> 7.82 us  [local(): lax.all_to_all(outgoing, HST_DEV, split_axis=0, concat_axis=0, tiled=True)]
    unnamed x20, local copies, waits for them, and re-layouts: 8.49 us -> 1.55 us
    all_to_all x1, waiting for transfers between devices: 0.01 us -> 3.04 us  [local(): recv = lax.all_to_all(halo, DEV, split_axis=0, concat_axis=0, tiled=True)]
    pallas_call x1 -> x0, local copies, waits for them, and re-layouts: 1.94 us -> none  [output(): pl.pallas_call(functools.partial(output_kernel, fanout=fanout), grid=(1,)...]
  transfers between devices with their start and end apart: 2 -> 2, of which waited for: 0 -> 2; matrix products, arithmetic and copies ran while one was open for 13% -> 12% of each run, Pallas kernels for 21% -> 18%
where the time goes in v2:
time: 128 us; the launch traced here: 127 us
  Pallas kernels  66.4 us (52%)
  blocking collectives  19.9 us (16%)
  local copies, waits for them, and re-layouts  15.3 us (12%)
  starting transfers between devices  14.7 us (11%)
  waiting for transfers between devices  10.9 us (9%)
    pallas_call x1, Pallas kernels, first_layer(): pl.pallas_call(functools.partial(first_layer_kernel, fanout=fanout), in_s...  28.2 us
    all_to_all x2, blocking collectives, sum_over(): lax.all_to_all(copies, axes, split_axis=0, concat_axis=0, tiled=True)  19.9 us
    pallas_call x1, Pallas kernels, counts(): pl.pallas_call(count_neighbours, grid=(rows // block,), in_specs=[pl.Bloc...  17.5 us
    gather x1, local copies, waits for them, and re-layouts, local(): hot_feat = hot_rows.at[hot_id].get(mode='promise_in_bounds')  13.7 us
    all_to_all x1, starting transfers between devices, local(): lax.all_to_all(outgoing, HST_DEV, split_axis=0, concat_axis=0, tiled=True)  11.2 us
    all_to_all x1, waiting for transfers between devices, local(): lax.all_to_all(outgoing, HST_DEV, split_axis=0, concat_axis=0, tiled=True)  7.82 us
    pallas_call x1, Pallas kernels, second_layer(): pl.pallas_call(functools.partial(second_layer_kernel, total_rows=total_ro...  7.78 us
    pallas_call x1, Pallas kernels, select_rows(): pl.pallas_call(select_rows_kernel, grid=(rows // BLOCK,), in_specs=[pl.Bl...  6.46 us
  transfers between devices with their start and end apart: 2, of which 2 were waited for; matrix products, arithmetic and copies ran while one was open for 12% of the time, Pallas kernels for 18%

profile of v2, /device:TPU:0, one launch (start us, length us, event | category | flops | bytes accessed | tf_op | source)
XLA Modules:
  0.0 127.4 jit_solution(13014779706850454072)
XLA Ops:
  0.0 6.5 %select_rows.1 = bf16[2048,768]{1,0:T(8,128)(2,1)} custom-call(s32[1,2048]{1,0:T(1,128)} %idx_ref.1, bf16[1024,768]{1,0:T(8,128)(2,1)} %table_ref.1), custom_call_target="tpu_custom_call" | custom-call | tf_op jit(solution)/shard_map/select_rows/pallas_call | solution.py:64
  6.5 0.0 copy-start.3
  6.5 0.0 copy-start.5
  6.5 11.2 %all-to-all-start = ((bf16[128,16,768]{2,1,0:T(8,128)(2,1)}), bf16[128,16,768]{2,1,0:T(8,128)(2,1)S(1)}, u32[]{:S(2)}, u32[]{:S(2)}) async-start(bf16[128,16,768]{2,1,0:T(8,128)(2,1)} %bitcast.15), calls=%async_computation | async-start | bytes 6291456 | tf_op jit(solution)/shard_map/all_to_all | solution.py:338
  17.6 0.0 copy-done.3
  17.7 1.4 %copy.21.adj_ref = s32[2048,15]{1,0:T(8,128)} copy(s32[2048,15]{0,1:T(8,128)S(1)} %copy-done.3) | data formatting | bytes 245760 | tf_op args[7]
  19.0 0.0 copy-done.5
  19.0 13.7 %gather_fusion = bf16[2048,768]{1,0:T(8,128)(2,1)} fusion(bf16[4096,768]{1,0:T(8,128)(2,1)} %param.16, s32[2048]{0:T(1024)S(1)} %fusion), kind=kCustom, calls=%fused_computation | custom fusion | bytes 6299648 | tf_op jit(solution)/shard_map/gather | solution.py:340
  32.7 0.0 copy-start.6
  32.7 0.0 copy-start.7
  32.7 0.0 copy-start.8
  32.7 17.5 %neighbour_counts.1.adj_hbm = bf16[2048,2048]{1,0:T(8,128)(2,1)} custom-call(s32[2048,15]{1,0:T(8,128)} %copy.21.adj_ref), custom_call_target="tpu_custom_call" | custom-call | flops 188743680 | bytes 8388608 | tf_op jit(solution)/shard_map/neighbour_counts/pallas_call | solution.py:104
  50.2 0.0 copy-done.6
  50.2 0.0 copy-done.7
  50.2 0.0 copy-done.8
  50.2 7.8 %all-to-all-done = bf16[128,16,768]{2,1,0:T(8,128)(2,1)S(1)} async-done(((bf16[128,16,768]{2,1,0:T(8,128)(2,1)}), bf16[128,16,768]{2,1,0:T(8,128)(2,1)S(1)}, u32[]{:S(2)}, u32[]{:S(2)}) %all-to-all-start) | async-done | bytes 3145760 | tf_op jit(solution)/shard_map/all_to_all | solution.py:338
  58.0 0.0 copy-start
  58.0 0.0 copy-start.1
  58.0 0.0 copy-start.2
  58.0 28.2 %first_layer.1 = (f32[2048,1024]{1,0:T(8,128)}, f32[2,1024]{1,0:T(2,128)S(1)}) custom-call(s32[1,2048]{1,0:T(1,128)S(1)} %bitcast.12, bf16[2048,768]{1,0:T(8,128)(2,1)S(1)} %bitcast.10, bf16[2048,768]{1,0:T(8,128)(2,1)} %gather_fusion, bf16[2048,2048]{1,0:T(8,128)(2,1)} %neighbour_counts.1.adj_hbm, bf16[768,1024]{1,0:T(8,128)(2,1)} %ws_hbm.1, ...), custom_call_target="tpu_custom_call" | custom-call | tf_op jit(solution)/shard_map/first_layer/pallas_call | solution.py:164
  86.3 8.5 %all_to_all.32 = f32[8,2,1024]{2,1,0:T(2,128)S(1)} all-to-all(f32[8,2,1024]{2,1,0:T(2,128)S(1)} %broadcast_in_dim.31), channel_id=1, replica_groups=mesh['hst_0'=4,'hst_1'=2,'dev_0'=4,'dev_1'=4] {'hst_0','hst_1'}, dimensions={0} | all-to-all | bytes 131072 | tf_op jit(solution)/shard_map/all_to_all | solution.py:311
  94.8 11.4 %all_to_all.33 = f32[16,2,1024]{2,1,0:T(2,128)S(1)} all-to-all(f32[16,2,1024]{2,1,0:T(2,128)S(1)} %broadcast_in_dim.32), channel_id=1, replica_groups=mesh['hst_0'=4,'hst_1'=2,'dev_0'=4,'dev_1'=4] {'dev_0','dev_1'}, dimensions={0} | all-to-all | bytes 262144 | tf_op jit(solution)/shard_map/all_to_all | solution.py:311
  106.2 0.1 reduce_sum.19.stat_ref
  106.3 0.0 copy-done
  106.3 0.0 copy-done.1
  106.3 0.0 copy-done.2
  106.3 0.0 copy-start.4
  106.3 7.8 %second_layer.1 = (f32[512,153]{1,0:T(8,128)}, bf16[2048,153]{1,0:T(8,128)(2,1)}, bf16[512,153]{1,0:T(8,128)(2,1)}) custom-call(f32[2048,1024]{1,0:T(8,128)} %get-tuple-element.12.pre_hbm, f32[2,1024]{1,0:T(2,128)S(1)} %reduce_sum.19.stat_ref, f32[1,1024]{1,0:T(1,128)S(1)} %bitcast.13, f32[1,1024]{1,0:T(1,128)S(1)} %bitcast.14, s32[1,512]{1,0:T(1,128)S(1)} %copy-done.2, ...), custom_call_target="tpu_custom_call" | custom-call | tf_op jit(solution)/shard_map/second_layer/pallas_call | solution.py:231
  114.1 3.5 %all-to-all-start.3 = ((bf16[16,32,153]{2,1,0:T(8,128)(2,1)}), bf16[16,32,153]{2,1,0:T(8,128)(2,1)S(1)}, u32[]{:S(2)}, u32[]{:S(2)}) async-start(bf16[16,32,153]{2,1,0:T(8,128)(2,1)} %bitcast.7), calls=%async_computation.3 | async-start | bytes 524288 | tf_op jit(solution)/shard_map/all_to_all | solution.py:356
  117.7 0.0 copy-done.4
  117.7 0.1 copy.24.adj_ref
  117.8 5.5 %targets_layer.1 = (f32[512,153]{1,0:T(8,128)S(1)}, bf16[512,512]{1,0:T(8,128)(2,1)S(1)}) custom-call(s32[512,15]{1,0:T(8,128)S(1)} %copy.24.adj_ref, f32[512,153]{1,0:T(8,128)} %get-tuple-element.14.own_hbm, bf16[2048,153]{1,0:T(8,128)(2,1)} %get-tuple-element.15.neigh_hbm), custom_call_target="tpu_custom_call" | custom-call | flops 58982400 | bytes 2097152 | tf_op jit(solution)/shard_map/targets_layer/pallas_call | solution.py:273
  123.3 3.0 %all-to-all-done.3 = bf16[16,32,153]{2,1,0:T(8,128)(2,1)S(1)} async-done(((bf16[16,32,153]{2,1,0:T(8,128)(2,1)}), bf16[16,32,153]{2,1,0:T(8,128)(2,1)S(1)}, u32[]{:S(2)}, u32[]{:S(2)}) %all-to-all-start.3) | async-done | bytes 156704 | tf_op jit(solution)/shard_map/all_to_all | solution.py:356
  126.3 1.1 output_layer.1
  (5 shorter events, 0.1 us)
Async XLA Ops:
  6.5 11.2 %copy-start.3 = (s32[2048,15]{0,1:T(8,128)S(1)}, s32[2048,15]{0,1:T(8,128)}, u32[]{:S(2)}) copy-start(s32[2048,15]{0,1:T(8,128)} %param.23) | copy-start | bytes 368644
  6.5 12.6 %copy-start.5 = (s32[2048]{0:T(1024)S(1)}, s32[2048]{0:T(1024)}, u32[]{:S(2)}) copy-start(s32[2048]{0:T(1024)} %param.19) | copy-start | bytes 24580
  6.5 51.6 %all-to-all-start = ((bf16[128,16,768]{2,1,0:T(8,128)(2,1)}), bf16[128,16,768]{2,1,0:T(8,128)(2,1)S(1)}, u32[]{:S(2)}, u32[]{:S(2)}) async-start(bf16[128,16,768]{2,1,0:T(8,128)(2,1)} %bitcast.15), calls=%async_computation | async-start | bytes 6291456 | tf_op jit(solution)/shard_map/all_to_all | solution.py:338
  32.7 17.5 %copy-start.6 = (s32[2048]{0:T(1024)S(1)}, s32[2048]{0:T(1024)}, u32[]{:S(2)}) copy-start(s32[2048]{0:T(1024)} %param.21) | copy-start | bytes 24580
  32.7 17.5 %copy-start.7 = (s32[2048]{0:T(1024)S(1)}, s32[2048]{0:T(1024)}, u32[]{:S(2)}) copy-start(s32[2048]{0:T(1024)} %param.20) | copy-start | bytes 24580
  32.7 17.5 %copy-start.8 = (s32[2048]{0:T(1024)S(1)}, s32[2048]{0:T(1024)}, u32[]{:S(2)}) copy-start(s32[2048]{0:T(1024)} %param.18) | copy-start | bytes 24580
  58.0 48.3 %copy-start = (f32[1024]{0:T(1024)S(1)}, f32[1024]{0:T(1024)}, u32[]{:S(2)}) copy-start(f32[1024]{0:T(1024)} %param.28) | copy-start | bytes 12292
  58.0 48.3 %copy-start.1 = (f32[1024]{0:T(1024)S(1)}, f32[1024]{0:T(1024)}, u32[]{:S(2)}) copy-start(f32[1024]{0:T(1024)} %param.29) | copy-start | bytes 12292
  58.0 48.3 %copy-start.2 = (s32[1,512]{1,0:T(1,128)S(1)}, s32[1,512]{1,0:T(1,128)}, u32[]{:S(2)}) copy-start(s32[1,512]{1,0:T(1,128)} %send_ref.1) | copy-start | bytes 6148
  106.3 11.4 %copy-start.4 = (s32[512,15]{0,1:T(8,128)S(1)}, s32[512,15]{0,1:T(8,128)}, u32[]{:S(2)}) copy-start(s32[512,15]{0,1:T(8,128)} %param.24) | copy-start | bytes 92164
  114.1 12.2 %all-to-all-start.3 = ((bf16[16,32,153]{2,1,0:T(8,128)(2,1)}), bf16[16,32,153]{2,1,0:T(8,128)(2,1)S(1)}, u32[]{:S(2)}, u32[]{:S(2)}) async-start(bf16[16,32,153]{2,1,0:T(8,128)(2,1)} %bitcast.7), calls=%async_computation.3 | async-start | bytes 524288 | tf_op jit(solution)/shard_map/all_to_all | solution.py:356

commit v3 on v2

--- a/solution.py
+++ b/solution.py
@@ -21,11 +21,10 @@
 
 
 def row_to_lanes(row):
-    return jnp.transpose(jnp.broadcast_to(row, (LANES, row.shape[1])))
-
-
-def one_hot(row, width):
-    spread = row_to_lanes(row).astype(jnp.int16)
+    return jnp.transpose(jnp.broadcast_to(row, (LANES, row.shape[1]))).astype(jnp.int16)
+
+
+def one_hot(spread, width):
     lane = lax.broadcasted_iota(jnp.int32, spread.shape, 1).astype(jnp.int16)
     one, zero = jnp.array(1, bf16), jnp.array(0, bf16)
     tiles = [
@@ -55,7 +54,7 @@
 
 
 def select_rows_kernel(idx_ref, table_ref, out_ref):
-    hot = one_hot(idx_ref[...], table_ref.shape[0])
+    hot = one_hot(row_to_lanes(idx_ref[...]), table_ref.shape[0])
     out_ref[...] = jnp.dot(hot, table_ref[...], preferred_element_type=f32).astype(bf16)
 
 
@@ -74,7 +73,7 @@
 
 def count_neighbours(adj_ref, out_ref):
     step = 16
-    group = 4
+    group = 8
     fanout = adj_ref.shape[1]
     width = out_ref.shape[1]
     lane = lax.broadcasted_iota(jnp.int32, (step, LANES), 1).astype(jnp.int16)
@@ -122,39 +121,41 @@
     rows, width = hot_ref.shape
     blocks = rows // BLOCK
     at = [pl.ds(b * BLOCK, BLOCK) for b in range(blocks)]
-    hot_in = [pltpu.make_async_copy(hot_hbm.at[at[b]], hot_ref.at[at[b]], hot_sem.at[b]) for b in range(blocks)]
-    adj_in = [pltpu.make_async_copy(adj_hbm.at[at[b]], adj_ref.at[at[b]], adj_sem.at[b]) for b in range(blocks)]
+    out = at[:-1] + [pl.ds(rows - BLOCK, BLOCK // 2), pl.ds(rows - BLOCK // 2, BLOCK // 2)]
+    hot_in = pltpu.make_async_copy(hot_hbm, hot_ref, hot_sem)
+    adj_in = pltpu.make_async_copy(adj_hbm, adj_ref, adj_sem)
     ws_in = pltpu.make_async_copy(ws_hbm, w_ref.at[pl.ds(0, width)], ws_sem)
     wn_in = pltpu.make_async_copy(wn_hbm, w_ref.at[pl.ds(width, width)], wn_sem)
-    pre_out = [pltpu.make_async_copy(pre_ref.at[b], pre_hbm.at[at[b]], pre_sem.at[b]) for b in range(blocks)]
-    for copy in hot_in + [ws_in, wn_in] + adj_in:
-        copy.start()
+    pre_out = [pltpu.make_async_copy(pre_ref.at[out[b]], pre_hbm.at[out[b]], pre_sem.at[b]) for b in range(len(out))]
+    hot_in.start()
     for b in range(blocks):
-        slot = slot_ref[:, at[b]]
-        cold = jnp.dot(one_hot(slot, arrived_ref.shape[0]), arrived_ref[...], preferred_element_type=f32)
-        is_hot = row_to_lanes(slot) < 0
-        hot_in[b].wait()
+        spread = row_to_lanes(slot_ref[:, at[b]])
+        cold = jnp.dot(one_hot(spread, arrived_ref.shape[0]), arrived_ref[...], preferred_element_type=f32).astype(bf16)
+        if b == 0:
+            hot_in.wait()
+            for copy in (adj_in, ws_in, wn_in):
+                copy.start()
         for j in range(width // LANES):
             lanes = slice(LANES * j, LANES * (j + 1))
-            both_ref[at[b], lanes] = jnp.where(is_hot, hot_ref[at[b], lanes].astype(f32), cold[:, lanes]).astype(bf16)
+            both_ref[at[b], lanes] = jnp.where(spread < jnp.int16(0), hot_ref[at[b], lanes], cold[:, lanes])
+    adj_in.wait()
+    ws_in.wait()
+    wn_in.wait()
     for b in range(blocks):
-        adj_in[b].wait()
         total = jnp.dot(adj_ref[at[b], :], both_ref[:, :width], preferred_element_type=f32)
         both_ref[at[b], width:] = (total * (1.0 / fanout)).astype(bf16)
-    ws_in.wait()
-    wn_in.wait()
     sums = squares = 0
-    for b in range(blocks):
-        pre = jnp.dot(both_ref[at[b], :], w_ref[...], preferred_element_type=f32)
-        pre_ref[b] = pre
+    for b in range(len(out)):
+        pre = jnp.dot(both_ref[out[b], :], w_ref[...], preferred_element_type=f32)
+        pre_ref[out[b], :] = pre
         pre_out[b].start()
-        grouped = pre.reshape(BLOCK // 8, 8, pre.shape[1])
+        grouped = pre.reshape(pre.shape[0] // 8, 8, pre.shape[1])
         sums = sums + jnp.sum(grouped, axis=0)
         squares = squares + jnp.sum(grouped * grouped, axis=0)
     stat_ref[0:1, :] = jnp.sum(sums, axis=0, keepdims=True)
     stat_ref[1:2, :] = jnp.sum(squares, axis=0, keepdims=True)
-    for b in range(blocks):
-        pre_out[b].wait()
+    for copy in pre_out:
+        copy.wait()
 
 
 def first_layer(slot, arrived, hot, adj, ws, wn, fanout):
@@ -173,12 +174,12 @@
             pltpu.VMEM(hot.shape, bf16),
             pltpu.VMEM((rows, rows), bf16),
             pltpu.VMEM((2 * width, hidden), bf16),
-            pltpu.VMEM((blocks, BLOCK, hidden), f32),
-            pltpu.SemaphoreType.DMA((blocks,)),
-            pltpu.SemaphoreType.DMA((blocks,)),
-            pltpu.SemaphoreType.DMA,
-            pltpu.SemaphoreType.DMA,
-            pltpu.SemaphoreType.DMA((blocks,)),
+            pltpu.VMEM((rows, hidden), f32),
+            pltpu.SemaphoreType.DMA,
+            pltpu.SemaphoreType.DMA,
+            pltpu.SemaphoreType.DMA,
+            pltpu.SemaphoreType.DMA,
+            pltpu.SemaphoreType.DMA((blocks + 1,)),
             pltpu.VMEM((rows, 2 * width), bf16),
         ],
         compiler_params=params(48),
@@ -217,7 +218,7 @@
             own_out.start()
         neigh_ref[at[b], :] = nt_dot(hidden, wn_ref[...]).astype(bf16)
     neigh_out.start()
-    pick = one_hot(send_ref[...], neigh_ref.shape[0])
+    pick = one_hot(row_to_lanes(send_ref[...]), neigh_ref.shape[0])
     halo_ref[...] = jnp.dot(pick, neigh_ref[...], preferred_element_type=f32).astype(bf16)
     own_out.wait()
     neigh_out.wait()

time: 128 us -> 124 us (0.969)
  Pallas kernels: 66.4 us -> 61.5 us
    pallas_call x1, Pallas kernels: 28.2 us -> 24.2 us  [first_layer(): pl.pallas_call(functools.partial(first_layer_kernel, fanout=fanout), in_s...]
where the time goes in v3:
time: 124 us; the launch traced here: 123 us
  Pallas kernels  61.5 us (50%)
  blocking collectives  19.9 us (16%)
  local copies, waits for them, and re-layouts  15.3 us (12%)
  starting transfers between devices  14.7 us (12%)
  waiting for transfers between devices  11.7 us (9%)
    pallas_call x1, Pallas kernels, first_layer(): pl.pallas_call(functools.partial(first_layer_kernel, fanout=fanout), in_s...  24.2 us
    all_to_all x2, blocking collectives, sum_over(): lax.all_to_all(copies, axes, split_axis=0, concat_axis=0, tiled=True)  19.9 us
    pallas_call x1, Pallas kernels, counts(): pl.pallas_call(count_neighbours, grid=(rows // block,), in_specs=[pl.Bloc...  16.7 us
    gather x1, local copies, waits for them, and re-layouts, local(): hot_feat = hot_rows.at[hot_id].get(mode='promise_in_bounds')  13.7 us
    all_to_all x1, starting transfers between devices, local(): lax.all_to_all(outgoing, HST_DEV, split_axis=0, concat_axis=0, tiled=True)  11.2 us
    all_to_all x1, waiting for transfers between devices, local(): lax.all_to_all(outgoing, HST_DEV, split_axis=0, concat_axis=0, tiled=True)  8.54 us
    pallas_call x1, Pallas kernels, second_layer(): pl.pallas_call(functools.partial(second_layer_kernel, total_rows=total_ro...  7.78 us
    pallas_call x1, Pallas kernels, select_rows(): pl.pallas_call(select_rows_kernel, grid=(rows // BLOCK,), in_specs=[pl.Bl...  6.46 us
  transfers between devices with their start and end apart: 2, of which 2 were waited for; matrix products, arithmetic and copies ran while one was open for 12% of the time, Pallas kernels for 18%

profile of v3, /device:TPU:0, one launch (start us, length us, event | category | flops | bytes accessed | tf_op | source)
XLA Modules:
  0.0 123.4 jit_solution(8639146605197520859)
XLA Ops:
  0.0 6.5 %select_rows.1 = bf16[2048,768]{1,0:T(8,128)(2,1)} custom-call(s32[1,2048]{1,0:T(1,128)} %idx_ref.1, bf16[1024,768]{1,0:T(8,128)(2,1)} %table_ref.1), custom_call_target="tpu_custom_call" | custom-call | tf_op jit(solution)/shard_map/select_rows/pallas_call | solution.py:63
  6.5 0.0 copy-start.3
  6.5 0.0 copy-start.5
  6.5 11.2 %all-to-all-start = ((bf16[128,16,768]{2,1,0:T(8,128)(2,1)}), bf16[128,16,768]{2,1,0:T(8,128)(2,1)S(1)}, u32[]{:S(2)}, u32[]{:S(2)}) async-start(bf16[128,16,768]{2,1,0:T(8,128)(2,1)} %bitcast.15), calls=%async_computation | async-start | bytes 6291456 | tf_op jit(solution)/shard_map/all_to_all | solution.py:339
  17.6 0.0 copy-done.3
  17.7 1.4 %copy.21.adj_ref = s32[2048,15]{1,0:T(8,128)} copy(s32[2048,15]{0,1:T(8,128)S(1)} %copy-done.3) | data formatting | bytes 245760 | tf_op args[7]
  19.0 0.0 copy-done.5
  19.0 13.7 %gather_fusion = bf16[2048,768]{1,0:T(8,128)(2,1)} fusion(bf16[4096,768]{1,0:T(8,128)(2,1)} %param.16, s32[2048]{0:T(1024)S(1)} %fusion), kind=kCustom, calls=%fused_computation | custom fusion | bytes 6299648 | tf_op jit(solution)/shard_map/gather | solution.py:341
  32.7 0.0 copy-start.6
  32.7 0.0 copy-start.7
  32.7 0.0 copy-start.8
  32.7 16.7 %neighbour_counts.1.adj_hbm = bf16[2048,2048]{1,0:T(8,128)(2,1)} custom-call(s32[2048,15]{1,0:T(8,128)} %copy.21.adj_ref), custom_call_target="tpu_custom_call" | custom-call | flops 188743680 | bytes 8388608 | tf_op jit(solution)/shard_map/neighbour_counts/pallas_call | solution.py:103
  49.5 0.0 copy-done.6
  49.5 0.0 copy-done.7
  49.5 0.0 copy-done.8
  49.5 8.5 %all-to-all-done = bf16[128,16,768]{2,1,0:T(8,128)(2,1)S(1)} async-done(((bf16[128,16,768]{2,1,0:T(8,128)(2,1)}), bf16[128,16,768]{2,1,0:T(8,128)(2,1)S(1)}, u32[]{:S(2)}, u32[]{:S(2)}) %all-to-all-start) | async-done | bytes 3145760 | tf_op jit(solution)/shard_map/all_to_all | solution.py:339
  58.0 0.0 copy-start
  58.0 0.0 copy-start.1
  58.0 0.0 copy-start.2
  58.0 24.2 %first_layer.1 = (f32[2048,1024]{1,0:T(8,128)}, f32[2,1024]{1,0:T(2,128)S(1)}) custom-call(s32[1,2048]{1,0:T(1,128)S(1)} %bitcast.12, bf16[2048,768]{1,0:T(8,128)(2,1)S(1)} %bitcast.10, bf16[2048,768]{1,0:T(8,128)(2,1)} %gather_fusion, bf16[2048,2048]{1,0:T(8,128)(2,1)} %neighbour_counts.1.adj_hbm, bf16[768,1024]{1,0:T(8,128)(2,1)} %ws_hbm.1, ...), custom_call_target="tpu_custom_call" | custom-call | tf_op jit(solution)/shard_map/first_layer/pallas_call | solution.py:165
  82.2 8.5 %all_to_all.32 = f32[8,2,1024]{2,1,0:T(2,128)S(1)} all-to-all(f32[8,2,1024]{2,1,0:T(2,128)S(1)} %broadcast_in_dim.31), channel_id=1, replica_groups=mesh['hst_0'=4,'hst_1'=2,'dev_0'=4,'dev_1'=4] {'hst_0','hst_1'}, dimensions={0} | all-to-all | bytes 131072 | tf_op jit(solution)/shard_map/all_to_all | solution.py:312
  90.8 11.4 %all_to_all.33 = f32[16,2,1024]{2,1,0:T(2,128)S(1)} all-to-all(f32[16,2,1024]{2,1,0:T(2,128)S(1)} %broadcast_in_dim.32), channel_id=1, replica_groups=mesh['hst_0'=4,'hst_1'=2,'dev_0'=4,'dev_1'=4] {'dev_0','dev_1'}, dimensions={0} | all-to-all | bytes 262144 | tf_op jit(solution)/shard_map/all_to_all | solution.py:312
  102.2 0.1 reduce_sum.19.stat_ref
  102.3 0.0 copy-done
  102.3 0.0 copy-done.1
  102.3 0.0 copy-done.2
  102.3 0.0 copy-start.4
  102.3 7.8 %second_layer.1 = (f32[512,153]{1,0:T(8,128)}, bf16[2048,153]{1,0:T(8,128)(2,1)}, bf16[512,153]{1,0:T(8,128)(2,1)}) custom-call(f32[2048,1024]{1,0:T(8,128)} %get-tuple-element.12.pre_hbm, f32[2,1024]{1,0:T(2,128)S(1)} %reduce_sum.19.stat_ref, f32[1,1024]{1,0:T(1,128)S(1)} %bitcast.13, f32[1,1024]{1,0:T(1,128)S(1)} %bitcast.14, s32[1,512]{1,0:T(1,128)S(1)} %copy-done.2, ...), custom_call_target="tpu_custom_call" | custom-call | tf_op jit(solution)/shard_map/second_layer/pallas_call | solution.py:232
  110.1 3.5 %all-to-all-start.3 = ((bf16[16,32,153]{2,1,0:T(8,128)(2,1)}), bf16[16,32,153]{2,1,0:T(8,128)(2,1)S(1)}, u32[]{:S(2)}, u32[]{:S(2)}) async-start(bf16[16,32,153]{2,1,0:T(8,128)(2,1)} %bitcast.7), calls=%async_computation.3 | async-start | bytes 524288 | tf_op jit(solution)/shard_map/all_to_all | solution.py:357
  113.7 0.0 copy-done.4
  113.7 0.1 copy.24.adj_ref
  113.8 5.3 %targets_layer.1 = (f32[512,153]{1,0:T(8,128)S(1)}, bf16[512,512]{1,0:T(8,128)(2,1)S(1)}) custom-call(s32[512,15]{1,0:T(8,128)S(1)} %copy.24.adj_ref, f32[512,153]{1,0:T(8,128)} %get-tuple-element.14.own_hbm, bf16[2048,153]{1,0:T(8,128)(2,1)} %get-tuple-element.15.neigh_hbm), custom_call_target="tpu_custom_call" | custom-call | flops 58982400 | bytes 2097152 | tf_op jit(solution)/shard_map/targets_layer/pallas_call | solution.py:274
  119.1 3.2 %all-to-all-done.3 = bf16[16,32,153]{2,1,0:T(8,128)(2,1)S(1)} async-done(((bf16[16,32,153]{2,1,0:T(8,128)(2,1)}), bf16[16,32,153]{2,1,0:T(8,128)(2,1)S(1)}, u32[]{:S(2)}, u32[]{:S(2)}) %all-to-all-start.3) | async-done | bytes 156704 | tf_op jit(solution)/shard_map/all_to_all | solution.py:357
  122.3 1.1 output_layer.1
  (5 shorter events, 0.1 us)
Async XLA Ops:
  6.5 11.2 %copy-start.3 = (s32[2048,15]{0,1:T(8,128)S(1)}, s32[2048,15]{0,1:T(8,128)}, u32[]{:S(2)}) copy-start(s32[2048,15]{0,1:T(8,128)} %param.23) | copy-start | bytes 368644
  6.5 12.6 %copy-start.5 = (s32[2048]{0:T(1024)S(1)}, s32[2048]{0:T(1024)}, u32[]{:S(2)}) copy-start(s32[2048]{0:T(1024)} %param.19) | copy-start | bytes 24580
  6.5 51.6 %all-to-all-start = ((bf16[128,16,768]{2,1,0:T(8,128)(2,1)}), bf16[128,16,768]{2,1,0:T(8,128)(2,1)S(1)}, u32[]{:S(2)}, u32[]{:S(2)}) async-start(bf16[128,16,768]{2,1,0:T(8,128)(2,1)} %bitcast.15), calls=%async_computation | async-start | bytes 6291456 | tf_op jit(solution)/shard_map/all_to_all | solution.py:339
  32.7 16.7 %copy-start.6 = (s32[2048]{0:T(1024)S(1)}, s32[2048]{0:T(1024)}, u32[]{:S(2)}) copy-start(s32[2048]{0:T(1024)} %param.21) | copy-start | bytes 24580
  32.7 16.7 %copy-start.7 = (s32[2048]{0:T(1024)S(1)}, s32[2048]{0:T(1024)}, u32[]{:S(2)}) copy-start(s32[2048]{0:T(1024)} %param.20) | copy-start | bytes 24580
  32.7 16.7 %copy-start.8 = (s32[2048]{0:T(1024)S(1)}, s32[2048]{0:T(1024)}, u32[]{:S(2)}) copy-start(s32[2048]{0:T(1024)} %param.18) | copy-start | bytes 24580
  58.0 44.3 %copy-start = (f32[1024]{0:T(1024)S(1)}, f32[1024]{0:T(1024)}, u32[]{:S(2)}) copy-start(f32[1024]{0:T(1024)} %param.28) | copy-start | bytes 12292
  58.0 44.3 %copy-start.1 = (f32[1024]{0:T(1024)S(1)}, f32[1024]{0:T(1024)}, u32[]{:S(2)}) copy-start(f32[1024]{0:T(1024)} %param.29) | copy-start | bytes 12292
  58.0 44.3 %copy-start.2 = (s32[1,512]{1,0:T(1,128)S(1)}, s32[1,512]{1,0:T(1,128)}, u32[]{:S(2)}) copy-start(s32[1,512]{1,0:T(1,128)} %send_ref.1) | copy-start | bytes 6148
  102.3 11.4 %copy-start.4 = (s32[512,15]{0,1:T(8,128)S(1)}, s32[512,15]{0,1:T(8,128)}, u32[]{:S(2)}) copy-start(s32[512,15]{0,1:T(8,128)} %param.24) | copy-start | bytes 92164
  110.1 12.2 %all-to-all-start.3 = ((bf16[16,32,153]{2,1,0:T(8,128)(2,1)}), bf16[16,32,153]{2,1,0:T(8,128)(2,1)S(1)}, u32[]{:S(2)}, u32[]{:S(2)}) async-start(bf16[16,32,153]{2,1,0:T(8,128)(2,1)} %bitcast.7), calls=%async_computation.3 | async-start | bytes 524288 | tf_op jit(solution)/shard_map/all_to_all | solution.py:357

commit v4 on v3

--- a/solution.py
+++ b/solution.py
@@ -53,19 +53,40 @@
     return pl.BlockSpec(shape, lambda i: (0,) * len(shape))
 
 
-def select_rows_kernel(idx_ref, table_ref, out_ref):
-    hot = one_hot(row_to_lanes(idx_ref[...]), table_ref.shape[0])
-    out_ref[...] = jnp.dot(hot, table_ref[...], preferred_element_type=f32).astype(bf16)
+def select_rows_kernel(idx_hbm, table_hbm, out_hbm, idx_ref, table_ref, out_ref, idx_sem, table_sem, out_sem):
+    blocks = out_ref.shape[0] // BLOCK
+    at = [pl.ds(b * BLOCK, BLOCK) for b in range(blocks)]
+    idx_in = pltpu.make_async_copy(idx_hbm, idx_ref, idx_sem)
+    table_in = pltpu.make_async_copy(table_hbm, table_ref, table_sem)
+    copies = [pltpu.make_async_copy(out_ref.at[at[b]], out_hbm.at[at[b]], out_sem.at[b]) for b in range(blocks)]
+    idx_in.start()
+    table_in.start()
+    idx_in.wait()
+    spread = [row_to_lanes(idx_ref[:, at[b]]) for b in range(blocks)]
+    table_in.wait()
+    for b in range(blocks):
+        pick = one_hot(spread[b], table_ref.shape[0])
+        out_ref[at[b], :] = jnp.dot(pick, table_ref[...], preferred_element_type=f32).astype(bf16)
+        copies[b].start()
+    for copy in copies:
+        copy.wait()
 
 
 def select_rows(idx, table):
     rows, width = idx.shape[1], table.shape[1]
     return pl.pallas_call(
         select_rows_kernel,
-        grid=(rows // BLOCK,),
-        in_specs=[pl.BlockSpec((1, BLOCK), lambda i: (0, i)), whole(table.shape)],
-        out_specs=pl.BlockSpec((BLOCK, width), lambda i: (i, 0)),
+        in_specs=[HBM, HBM],
+        out_specs=HBM,
         out_shape=pltpu.HBM((rows, width), bf16),
+        scratch_shapes=[
+            pltpu.VMEM(idx.shape, jnp.int32),
+            pltpu.VMEM(table.shape, bf16),
+            pltpu.VMEM((rows, width), bf16),
+            pltpu.SemaphoreType.DMA,
+            pltpu.SemaphoreType.DMA,
+            pltpu.SemaphoreType.DMA((rows // BLOCK,)),
+        ],
         compiler_params=params(24),
         name="select_rows",
     )(in_hbm(idx), in_hbm(table))
@@ -195,30 +216,35 @@
     pre_hbm, stat_ref, gain_ref, shift_ref, send_ref, ws_hbm, wn_hbm, own_hbm, neigh_hbm, halo_ref,
     pre_ref, ws_ref, wn_ref, own_ref, neigh_ref, pre_sem, ws_sem, wn_sem, own_sem, neigh_sem, *, total_rows
 ):
-    blocks = pre_ref.shape[0] // BLOCK
-    at = [pl.ds(b * BLOCK, BLOCK) for b in range(blocks)]
-    pre_in = [pltpu.make_async_copy(pre_hbm.at[at[b]], pre_ref.at[at[b]], pre_sem.at[b]) for b in range(blocks)]
+    step = BLOCK // 2
+    at = [pl.ds(start, step) for start in range(0, pre_ref.shape[0], step)]
+    pre_in = [pltpu.make_async_copy(pre_hbm.at[rows], pre_ref.at[rows], pre_sem.at[b]) for b, rows in enumerate(at)]
     ws_in = pltpu.make_async_copy(ws_hbm, ws_ref, ws_sem)
     wn_in = pltpu.make_async_copy(wn_hbm, wn_ref, wn_sem)
     own_out = pltpu.make_async_copy(own_ref, own_hbm, own_sem)
     neigh_out = pltpu.make_async_copy(neigh_ref, neigh_hbm, neigh_sem)
-    for copy in [pre_in[0], wn_in, ws_in] + pre_in[1:]:
+    for copy in [wn_in] + pre_in[:3] + [ws_in]:
         copy.start()
+    spread = row_to_lanes(send_ref[...])
     mean = stat_ref[0:1, :] * (1.0 / total_rows)
     variance = stat_ref[1:2, :] * (1.0 / total_rows) - mean * mean
     scale = lax.rsqrt(variance + epsilon) * gain_ref[...]
     shift = shift_ref[...]
-    for b in range(blocks):
+    for b, rows in enumerate(at):
         pre_in[b].wait()
-        hidden = jnp.maximum((pre_ref[at[b], :] - mean) * scale + shift, 0.0).astype(bf16)
+        if b + 3 < len(at):
+            pre_in[b + 3].start()
+        hidden = jnp.maximum((pre_ref[rows, :] - mean) * scale + shift, 0.0).astype(bf16)
         if b == 0:
             wn_in.wait()
             ws_in.wait()
-            own_ref[...] = nt_dot(hidden, ws_ref[...])
+        neigh_ref[rows, :] = nt_dot(hidden, wn_ref[...]).astype(bf16)
+        if b < 2:
+            own_ref[rows, :] = nt_dot(hidden, ws_ref[...])
+        if b == 2 - 1:
             own_out.start()
-        neigh_ref[at[b], :] = nt_dot(hidden, wn_ref[...]).astype(bf16)
     neigh_out.start()
-    pick = one_hot(row_to_lanes(send_ref[...]), neigh_ref.shape[0])
+    pick = one_hot(spread, neigh_ref.shape[0])
     halo_ref[...] = jnp.dot(pick, neigh_ref[...], preferred_element_type=f32).astype(bf16)
     own_out.wait()
     neigh_out.wait()
@@ -244,7 +270,7 @@
             pltpu.VMEM(wn.shape, bf16),
             pltpu.VMEM((BLOCK, classes), f32),
             pltpu.VMEM((rows, classes), bf16),
-            dma((rows // BLOCK,)),
+            dma((rows // (BLOCK // 2),)),
             dma,
             dma,
             dma,

time: 124 us -> 123 us (level)
  no operation moved by 1% of the time
where the time goes in v4:
time: 123 us
  Pallas kernels  60.7 us (49%)
  blocking collectives  19.9 us (16%)
  local copies, waits for them, and re-layouts  15.3 us (12%)
  starting transfers between devices  14.7 us (12%)
  waiting for transfers between devices  11.7 us (10%)
    pallas_call x1, Pallas kernels, first_layer(): pl.pallas_call(functools.partial(first_layer_kernel, fanout=fanout), in_s...  24.2 us
    all_to_all x2, blocking collectives, sum_over(): lax.all_to_all(copies, axes, split_axis=0, concat_axis=0, tiled=True)  19.9 us
    pallas_call x1, Pallas kernels, counts(): pl.pallas_call(count_neighbours, grid=(rows // block,), in_specs=[pl.Bloc...  16.7 us
    gather x1, local copies, waits for them, and re-layouts, local(): hot_feat = hot_rows.at[hot_id].get(mode='promise_in_bounds')  13.7 us
    all_to_all x1, starting transfers between devices, local(): lax.all_to_all(outgoing, HST_DEV, split_axis=0, concat_axis=0, tiled=True)  11.2 us
    all_to_all x1, waiting for transfers between devices, local(): lax.all_to_all(outgoing, HST_DEV, split_axis=0, concat_axis=0, tiled=True)  8.54 us
    pallas_call x1, Pallas kernels, second_layer(): pl.pallas_call(functools.partial(second_layer_kernel, total_rows=total_ro...  7.54 us
    pallas_call x1, Pallas kernels, select_rows(): pl.pallas_call(select_rows_kernel, in_specs=[HBM, HBM], out_specs=HBM, ou...  5.84 us
  transfers between devices with their start and end apart: 2, of which 2 were waited for; matrix products, arithmetic and copies ran while one was open for 12% of the time, Pallas kernels for 18%

profile of v4, /device:TPU:0, one launch (start us, length us, event | category | flops | bytes accessed | tf_op | source)
XLA Modules:
  0.0 122.6 jit_solution(9521411446817680564)
XLA Ops:
  0.0 5.8 %select_rows.1 = bf16[2048,768]{1,0:T(8,128)(2,1)} custom-call(s32[1,2048]{1,0:T(1,128)} %idx_hbm.1, bf16[1024,768]{1,0:T(8,128)(2,1)} %table_hbm.1), custom_call_target="tpu_custom_call" | custom-call | tf_op jit(solution)/shard_map/select_rows/pallas_call | solution.py:77
  5.9 0.0 copy-start.3
  5.9 0.0 copy-start.5
  5.9 11.2 %all-to-all-start = ((bf16[128,16,768]{2,1,0:T(8,128)(2,1)}), bf16[128,16,768]{2,1,0:T(8,128)(2,1)S(1)}, u32[]{:S(2)}, u32[]{:S(2)}) async-start(bf16[128,16,768]{2,1,0:T(8,128)(2,1)} %bitcast.15), calls=%async_computation | async-start | bytes 6291456 | tf_op jit(solution)/shard_map/all_to_all | solution.py:365
  17.1 0.0 copy-done.3
  17.1 1.4 %copy.21.adj_ref = s32[2048,15]{1,0:T(8,128)} copy(s32[2048,15]{0,1:T(8,128)S(1)} %copy-done.3) | data formatting | bytes 245760 | tf_op args[7]
  18.4 0.0 copy-done.5
  18.4 13.7 %gather_fusion = bf16[2048,768]{1,0:T(8,128)(2,1)} fusion(bf16[4096,768]{1,0:T(8,128)(2,1)} %param.16, s32[2048]{0:T(1024)S(1)} %fusion), kind=kCustom, calls=%fused_computation | custom fusion | bytes 6299648 | tf_op jit(solution)/shard_map/gather | solution.py:367
  32.1 0.0 copy-start.6
  32.1 0.0 copy-start.7
  32.1 0.0 copy-start.8
  32.1 16.7 %neighbour_counts.1.adj_hbm = bf16[2048,2048]{1,0:T(8,128)(2,1)} custom-call(s32[2048,15]{1,0:T(8,128)} %copy.21.adj_ref), custom_call_target="tpu_custom_call" | custom-call | flops 188743680 | bytes 8388608 | tf_op jit(solution)/shard_map/neighbour_counts/pallas_call | solution.py:124
  48.9 0.0 copy-done.6
  48.9 0.0 copy-done.7
  48.9 0.0 copy-done.8
  48.9 8.5 %all-to-all-done = bf16[128,16,768]{2,1,0:T(8,128)(2,1)S(1)} async-done(((bf16[128,16,768]{2,1,0:T(8,128)(2,1)}), bf16[128,16,768]{2,1,0:T(8,128)(2,1)S(1)}, u32[]{:S(2)}, u32[]{:S(2)}) %all-to-all-start) | async-done | bytes 3145760 | tf_op jit(solution)/shard_map/all_to_all | solution.py:365
  57.4 0.0 copy-start
  57.4 0.0 copy-start.1
  57.4 0.0 copy-start.2
  57.4 24.2 %first_layer.1 = (f32[2048,1024]{1,0:T(8,128)}, f32[2,1024]{1,0:T(2,128)S(1)}) custom-call(s32[1,2048]{1,0:T(1,128)S(1)} %bitcast.12, bf16[2048,768]{1,0:T(8,128)(2,1)S(1)} %bitcast.10, bf16[2048,768]{1,0:T(8,128)(2,1)} %gather_fusion, bf16[2048,2048]{1,0:T(8,128)(2,1)} %neighbour_counts.1.adj_hbm, bf16[768,1024]{1,0:T(8,128)(2,1)} %ws_hbm.1, ...), custom_call_target="tpu_custom_call" | custom-call | tf_op jit(solution)/shard_map/first_layer/pallas_call | solution.py:186
  81.7 8.5 %all_to_all.32 = f32[8,2,1024]{2,1,0:T(2,128)S(1)} all-to-all(f32[8,2,1024]{2,1,0:T(2,128)S(1)} %broadcast_in_dim.31), channel_id=1, replica_groups=mesh['hst_0'=4,'hst_1'=2,'dev_0'=4,'dev_1'=4] {'hst_0','hst_1'}, dimensions={0} | all-to-all | bytes 131072 | tf_op jit(solution)/shard_map/all_to_all | solution.py:338
  90.2 11.4 %all_to_all.33 = f32[16,2,1024]{2,1,0:T(2,128)S(1)} all-to-all(f32[16,2,1024]{2,1,0:T(2,128)S(1)} %broadcast_in_dim.32), channel_id=1, replica_groups=mesh['hst_0'=4,'hst_1'=2,'dev_0'=4,'dev_1'=4] {'dev_0','dev_1'}, dimensions={0} | all-to-all | bytes 262144 | tf_op jit(solution)/shard_map/all_to_all | solution.py:338
  101.6 0.1 reduce_sum.19.stat_ref
  101.7 0.0 copy-done
  101.7 0.0 copy-done.1
  101.7 0.0 copy-done.2
  101.7 0.0 copy-start.4
  101.7 7.5 %second_layer.1 = (f32[512,153]{1,0:T(8,128)}, bf16[2048,153]{1,0:T(8,128)(2,1)}, bf16[512,153]{1,0:T(8,128)(2,1)}) custom-call(f32[2048,1024]{1,0:T(8,128)} %get-tuple-element.12.pre_hbm, f32[2,1024]{1,0:T(2,128)S(1)} %reduce_sum.19.stat_ref, f32[1,1024]{1,0:T(1,128)S(1)} %bitcast.13, f32[1,1024]{1,0:T(1,128)S(1)} %bitcast.14, s32[1,512]{1,0:T(1,128)S(1)} %copy-done.2, ...), custom_call_target="tpu_custom_call" | custom-call | tf_op jit(solution)/shard_map/second_layer/pallas_call | solution.py:258
  109.3 3.5 %all-to-all-start.3 = ((bf16[16,32,153]{2,1,0:T(8,128)(2,1)}), bf16[16,32,153]{2,1,0:T(8,128)(2,1)S(1)}, u32[]{:S(2)}, u32[]{:S(2)}) async-start(bf16[16,32,153]{2,1,0:T(8,128)(2,1)} %bitcast.7), calls=%async_computation.3 | async-start | bytes 524288 | tf_op jit(solution)/shard_map/all_to_all | solution.py:383
  112.8 0.0 copy-done.4
  112.8 0.1 copy.24.adj_ref
  113.0 5.3 %targets_layer.1 = (f32[512,153]{1,0:T(8,128)S(1)}, bf16[512,512]{1,0:T(8,128)(2,1)S(1)}) custom-call(s32[512,15]{1,0:T(8,128)S(1)} %copy.24.adj_ref, f32[512,153]{1,0:T(8,128)} %get-tuple-element.14.own_hbm, bf16[2048,153]{1,0:T(8,128)(2,1)} %get-tuple-element.15.neigh_hbm), custom_call_target="tpu_custom_call" | custom-call | flops 58982400 | bytes 2097152 | tf_op jit(solution)/shard_map/targets_layer/pallas_call | solution.py:300
  118.3 3.2 %all-to-all-done.3 = bf16[16,32,153]{2,1,0:T(8,128)(2,1)S(1)} async-done(((bf16[16,32,153]{2,1,0:T(8,128)(2,1)}), bf16[16,32,153]{2,1,0:T(8,128)(2,1)S(1)}, u32[]{:S(2)}, u32[]{:S(2)}) %all-to-all-start.3) | async-done | bytes 156704 | tf_op jit(solution)/shard_map/all_to_all | solution.py:383
  121.5 1.1 output_layer.1
  (5 shorter events, 0.1 us)
Async XLA Ops:
  5.9 11.2 %copy-start.3 = (s32[2048,15]{0,1:T(8,128)S(1)}, s32[2048,15]{0,1:T(8,128)}, u32[]{:S(2)}) copy-start(s32[2048,15]{0,1:T(8,128)} %param.23) | copy-start | bytes 368644
  5.9 12.6 %copy-start.5 = (s32[2048]{0:T(1024)S(1)}, s32[2048]{0:T(1024)}, u32[]{:S(2)}) copy-start(s32[2048]{0:T(1024)} %param.19) | copy-start | bytes 24580
  5.9 51.6 %all-to-all-start = ((bf16[128,16,768]{2,1,0:T(8,128)(2,1)}), bf16[128,16,768]{2,1,0:T(8,128)(2,1)S(1)}, u32[]{:S(2)}, u32[]{:S(2)}) async-start(bf16[128,16,768]{2,1,0:T(8,128)(2,1)} %bitcast.15), calls=%async_computation | async-start | bytes 6291456 | tf_op jit(solution)/shard_map/all_to_all | solution.py:365
  32.1 16.7 %copy-start.6 = (s32[2048]{0:T(1024)S(1)}, s32[2048]{0:T(1024)}, u32[]{:S(2)}) copy-start(s32[2048]{0:T(1024)} %param.21) | copy-start | bytes 24580
  32.1 16.7 %copy-start.7 = (s32[2048]{0:T(1024)S(1)}, s32[2048]{0:T(1024)}, u32[]{:S(2)}) copy-start(s32[2048]{0:T(1024)} %param.20) | copy-start | bytes 24580
  32.1 16.7 %copy-start.8 = (s32[2048]{0:T(1024)S(1)}, s32[2048]{0:T(1024)}, u32[]{:S(2)}) copy-start(s32[2048]{0:T(1024)} %param.18) | copy-start | bytes 24580
  57.4 44.3 %copy-start = (f32[1024]{0:T(1024)S(1)}, f32[1024]{0:T(1024)}, u32[]{:S(2)}) copy-start(f32[1024]{0:T(1024)} %param.28) | copy-start | bytes 12292
  57.4 44.3 %copy-start.1 = (f32[1024]{0:T(1024)S(1)}, f32[1024]{0:T(1024)}, u32[]{:S(2)}) copy-start(f32[1024]{0:T(1024)} %param.29) | copy-start | bytes 12292
  57.4 44.3 %copy-start.2 = (s32[1,512]{1,0:T(1,128)S(1)}, s32[1,512]{1,0:T(1,128)}, u32[]{:S(2)}) copy-start(s32[1,512]{1,0:T(1,128)} %send_ref.1) | copy-start | bytes 6148
  101.7 11.1 %copy-start.4 = (s32[512,15]{0,1:T(8,128)S(1)}, s32[512,15]{0,1:T(8,128)}, u32[]{:S(2)}) copy-start(s32[512,15]{0,1:T(8,128)} %param.24) | copy-start | bytes 92164
  109.3 12.2 %all-to-all-start.3 = ((bf16[16,32,153]{2,1,0:T(8,128)(2,1)}), bf16[16,32,153]{2,1,0:T(8,128)(2,1)S(1)}, u32[]{:S(2)}, u32[]{:S(2)}) async-start(bf16[16,32,153]{2,1,0:T(8,128)(2,1)} %bitcast.7), calls=%async_computation.3 | async-start | bytes 524288 | tf_op jit(solution)/shard_map/all_to_all | solution.py:383

commit v5 on v4

--- a/solution.py
+++ b/solution.py
@@ -148,14 +148,13 @@
     ws_in = pltpu.make_async_copy(ws_hbm, w_ref.at[pl.ds(0, width)], ws_sem)
     wn_in = pltpu.make_async_copy(wn_hbm, w_ref.at[pl.ds(width, width)], wn_sem)
     pre_out = [pltpu.make_async_copy(pre_ref.at[out[b]], pre_hbm.at[out[b]], pre_sem.at[b]) for b in range(len(out))]
-    hot_in.start()
+    for copy in (hot_in, adj_in, ws_in, wn_in):
+        copy.start()
     for b in range(blocks):
         spread = row_to_lanes(slot_ref[:, at[b]])
         cold = jnp.dot(one_hot(spread, arrived_ref.shape[0]), arrived_ref[...], preferred_element_type=f32).astype(bf16)
         if b == 0:
             hot_in.wait()
-            for copy in (adj_in, ws_in, wn_in):
-                copy.start()
         for j in range(width // LANES):
             lanes = slice(LANES * j, LANES * (j + 1))
             both_ref[at[b], lanes] = jnp.where(spread < jnp.int16(0), hot_ref[at[b], lanes], cold[:, lanes])

time: 123 us -> 122 us (level)
  Pallas kernels: 60.7 us -> 59.2 us
    pallas_call x1, Pallas kernels: 24.2 us -> 22.7 us  [first_layer(): pl.pallas_call(functools.partial(first_layer_kernel, fanout=fanout), in_s...]
  transfers between devices with their start and end apart: 2 -> 2, of which waited for: 2 -> 2; matrix products, arithmetic and copies ran while one was open for 12% -> 13% of each run, Pallas kernels for 18% -> 18%
where the time goes in v5:
time: 122 us; the launch traced here: 121 us
  Pallas kernels  59.2 us (49%)
  blocking collectives  19.9 us (16%)
  local copies, waits for them, and re-layouts  15.3 us (13%)
  starting transfers between devices  14.7 us (12%)
  waiting for transfers between devices  11.7 us (10%)
    pallas_call x1, Pallas kernels, first_layer(): pl.pallas_call(functools.partial(first_layer_kernel, fanout=fanout), in_s...  22.7 us
    all_to_all x2, blocking collectives, sum_over(): lax.all_to_all(copies, axes, split_axis=0, concat_axis=0, tiled=True)  19.9 us
    pallas_call x1, Pallas kernels, counts(): pl.pallas_call(count_neighbours, grid=(rows // block,), in_specs=[pl.Bloc...  16.7 us
    gather x1, local copies, waits for them, and re-layouts, local(): hot_feat = hot_rows.at[hot_id].get(mode='promise_in_bounds')  13.7 us
    all_to_all x1, starting transfers between devices, local(): lax.all_to_all(outgoing, HST_DEV, split_axis=0, concat_axis=0, tiled=True)  11.2 us
    all_to_all x1, waiting for transfers between devices, local(): lax.all_to_all(outgoing, HST_DEV, split_axis=0, concat_axis=0, tiled=True)  8.54 us
    pallas_call x1, Pallas kernels, second_layer(): pl.pallas_call(functools.partial(second_layer_kernel, total_rows=total_ro...  7.53 us
    pallas_call x1, Pallas kernels, select_rows(): pl.pallas_call(select_rows_kernel, in_specs=[HBM, HBM], out_specs=HBM, ou...  5.84 us
  transfers between devices with their start and end apart: 2, of which 2 were waited for; matrix products, arithmetic and copies ran while one was open for 13% of the time, Pallas kernels for 18%

profile of v5, /device:TPU:0, one launch (start us, length us, event | category | flops | bytes accessed | tf_op | source)
XLA Modules:
  0.0 121.1 jit_solution(16529724953395380590)
XLA Ops:
  0.0 5.8 %select_rows.1 = bf16[2048,768]{1,0:T(8,128)(2,1)} custom-call(s32[1,2048]{1,0:T(1,128)} %idx_hbm.1, bf16[1024,768]{1,0:T(8,128)(2,1)} %table_hbm.1), custom_call_target="tpu_custom_call" | custom-call | tf_op jit(solution)/shard_map/select_rows/pallas_call | solution.py:77
  5.9 0.0 copy-start.3
  5.9 0.0 copy-start.5
  5.9 11.2 %all-to-all-start = ((bf16[128,16,768]{2,1,0:T(8,128)(2,1)}), bf16[128,16,768]{2,1,0:T(8,128)(2,1)S(1)}, u32[]{:S(2)}, u32[]{:S(2)}) async-start(bf16[128,16,768]{2,1,0:T(8,128)(2,1)} %bitcast.15), calls=%async_computation | async-start | bytes 6291456 | tf_op jit(solution)/shard_map/all_to_all | solution.py:364
  17.1 0.0 copy-done.3
  17.1 1.4 %copy.21.adj_ref = s32[2048,15]{1,0:T(8,128)} copy(s32[2048,15]{0,1:T(8,128)S(1)} %copy-done.3) | data formatting | bytes 245760 | tf_op args[7]
  18.4 0.0 copy-done.5
  18.4 13.7 %gather_fusion = bf16[2048,768]{1,0:T(8,128)(2,1)} fusion(bf16[4096,768]{1,0:T(8,128)(2,1)} %param.16, s32[2048]{0:T(1024)S(1)} %fusion), kind=kCustom, calls=%fused_computation | custom fusion | bytes 6299648 | tf_op jit(solution)/shard_map/gather | solution.py:366
  32.1 0.0 copy-start.6
  32.1 0.0 copy-start.7
  32.1 0.0 copy-start.8
  32.1 16.7 %neighbour_counts.1.adj_hbm = bf16[2048,2048]{1,0:T(8,128)(2,1)} custom-call(s32[2048,15]{1,0:T(8,128)} %copy.21.adj_ref), custom_call_target="tpu_custom_call" | custom-call | flops 188743680 | bytes 8388608 | tf_op jit(solution)/shard_map/neighbour_counts/pallas_call | solution.py:124
  48.9 0.0 copy-done.6
  48.9 0.0 copy-done.7
  48.9 0.0 copy-done.8
  48.9 8.5 %all-to-all-done = bf16[128,16,768]{2,1,0:T(8,128)(2,1)S(1)} async-done(((bf16[128,16,768]{2,1,0:T(8,128)(2,1)}), bf16[128,16,768]{2,1,0:T(8,128)(2,1)S(1)}, u32[]{:S(2)}, u32[]{:S(2)}) %all-to-all-start) | async-done | bytes 3145760 | tf_op jit(solution)/shard_map/all_to_all | solution.py:364
  57.4 0.0 copy-start
  57.4 0.0 copy-start.1
  57.4 0.0 copy-start.2
  57.4 22.7 %first_layer.1 = (f32[2048,1024]{1,0:T(8,128)}, f32[2,1024]{1,0:T(2,128)S(1)}) custom-call(s32[1,2048]{1,0:T(1,128)S(1)} %bitcast.12, bf16[2048,768]{1,0:T(8,128)(2,1)S(1)} %bitcast.10, bf16[2048,768]{1,0:T(8,128)(2,1)} %gather_fusion, bf16[2048,2048]{1,0:T(8,128)(2,1)} %neighbour_counts.1.adj_hbm, bf16[768,1024]{1,0:T(8,128)(2,1)} %ws_hbm.1, ...), custom_call_target="tpu_custom_call" | custom-call | tf_op jit(solution)/shard_map/first_layer/pallas_call | solution.py:185
  80.2 8.5 %all_to_all.32 = f32[8,2,1024]{2,1,0:T(2,128)S(1)} all-to-all(f32[8,2,1024]{2,1,0:T(2,128)S(1)} %broadcast_in_dim.31), channel_id=1, replica_groups=mesh['hst_0'=4,'hst_1'=2,'dev_0'=4,'dev_1'=4] {'hst_0','hst_1'}, dimensions={0} | all-to-all | bytes 131072 | tf_op jit(solution)/shard_map/all_to_all | solution.py:337
  88.7 11.4 %all_to_all.33 = f32[16,2,1024]{2,1,0:T(2,128)S(1)} all-to-all(f32[16,2,1024]{2,1,0:T(2,128)S(1)} %broadcast_in_dim.32), channel_id=1, replica_groups=mesh['hst_0'=4,'hst_1'=2,'dev_0'=4,'dev_1'=4] {'dev_0','dev_1'}, dimensions={0} | all-to-all | bytes 262144 | tf_op jit(solution)/shard_map/all_to_all | solution.py:337
  100.2 0.1 reduce_sum.19.stat_ref
  100.2 0.0 copy-done
  100.2 0.0 copy-done.1
  100.2 0.0 copy-done.2
  100.2 0.0 copy-start.4
  100.3 7.5 %second_layer.1 = (f32[512,153]{1,0:T(8,128)}, bf16[2048,153]{1,0:T(8,128)(2,1)}, bf16[512,153]{1,0:T(8,128)(2,1)}) custom-call(f32[2048,1024]{1,0:T(8,128)} %get-tuple-element.12.pre_hbm, f32[2,1024]{1,0:T(2,128)S(1)} %reduce_sum.19.stat_ref, f32[1,1024]{1,0:T(1,128)S(1)} %bitcast.13, f32[1,1024]{1,0:T(1,128)S(1)} %bitcast.14, s32[1,512]{1,0:T(1,128)S(1)} %copy-done.2, ...), custom_call_target="tpu_custom_call" | custom-call | tf_op jit(solution)/shard_map/second_layer/pallas_call | solution.py:257
  107.8 3.5 %all-to-all-start.3 = ((bf16[16,32,153]{2,1,0:T(8,128)(2,1)}), bf16[16,32,153]{2,1,0:T(8,128)(2,1)S(1)}, u32[]{:S(2)}, u32[]{:S(2)}) async-start(bf16[16,32,153]{2,1,0:T(8,128)(2,1)} %bitcast.7), calls=%async_computation.3 | async-start | bytes 524288 | tf_op jit(solution)/shard_map/all_to_all | solution.py:382
  111.4 0.0 copy-done.4
  111.4 0.1 copy.24.adj_ref
  111.5 5.3 %targets_layer.1 = (f32[512,153]{1,0:T(8,128)S(1)}, bf16[512,512]{1,0:T(8,128)(2,1)S(1)}) custom-call(s32[512,15]{1,0:T(8,128)S(1)} %copy.24.adj_ref, f32[512,153]{1,0:T(8,128)} %get-tuple-element.14.own_hbm, bf16[2048,153]{1,0:T(8,128)(2,1)} %get-tuple-element.15.neigh_hbm), custom_call_target="tpu_custom_call" | custom-call | flops 58982400 | bytes 2097152 | tf_op jit(solution)/shard_map/targets_layer/pallas_call | solution.py:299
  116.8 3.2 %all-to-all-done.3 = bf16[16,32,153]{2,1,0:T(8,128)(2,1)S(1)} async-done(((bf16[16,32,153]{2,1,0:T(8,128)(2,1)}), bf16[16,32,153]{2,1,0:T(8,128)(2,1)S(1)}, u32[]{:S(2)}, u32[]{:S(2)}) %all-to-all-start.3) | async-done | bytes 156704 | tf_op jit(solution)/shard_map/all_to_all | solution.py:382
  120.0 1.1 output_layer.1
  (5 shorter events, 0.1 us)
Async XLA Ops:
  5.9 11.2 %copy-start.3 = (s32[2048,15]{0,1:T(8,128)S(1)}, s32[2048,15]{0,1:T(8,128)}, u32[]{:S(2)}) copy-start(s32[2048,15]{0,1:T(8,128)} %param.23) | copy-start | bytes 368644
  5.9 12.6 %copy-start.5 = (s32[2048]{0:T(1024)S(1)}, s32[2048]{0:T(1024)}, u32[]{:S(2)}) copy-start(s32[2048]{0:T(1024)} %param.19) | copy-start | bytes 24580
  5.9 51.6 %all-to-all-start = ((bf16[128,16,768]{2,1,0:T(8,128)(2,1)}), bf16[128,16,768]{2,1,0:T(8,128)(2,1)S(1)}, u32[]{:S(2)}, u32[]{:S(2)}) async-start(bf16[128,16,768]{2,1,0:T(8,128)(2,1)} %bitcast.15), calls=%async_computation | async-start | bytes 6291456 | tf_op jit(solution)/shard_map/all_to_all | solution.py:364
  32.1 16.7 %copy-start.6 = (s32[2048]{0:T(1024)S(1)}, s32[2048]{0:T(1024)}, u32[]{:S(2)}) copy-start(s32[2048]{0:T(1024)} %param.21) | copy-start | bytes 24580
  32.1 16.7 %copy-start.7 = (s32[2048]{0:T(1024)S(1)}, s32[2048]{0:T(1024)}, u32[]{:S(2)}) copy-start(s32[2048]{0:T(1024)} %param.20) | copy-start | bytes 24580
  32.1 16.7 %copy-start.8 = (s32[2048]{0:T(1024)S(1)}, s32[2048]{0:T(1024)}, u32[]{:S(2)}) copy-start(s32[2048]{0:T(1024)} %param.18) | copy-start | bytes 24580
  57.4 42.8 %copy-start = (f32[1024]{0:T(1024)S(1)}, f32[1024]{0:T(1024)}, u32[]{:S(2)}) copy-start(f32[1024]{0:T(1024)} %param.28) | copy-start | bytes 12292
  57.4 42.8 %copy-start.1 = (f32[1024]{0:T(1024)S(1)}, f32[1024]{0:T(1024)}, u32[]{:S(2)}) copy-start(f32[1024]{0:T(1024)} %param.29) | copy-start | bytes 12292
  57.4 42.8 %copy-start.2 = (s32[1,512]{1,0:T(1,128)S(1)}, s32[1,512]{1,0:T(1,128)}, u32[]{:S(2)}) copy-start(s32[1,512]{1,0:T(1,128)} %send_ref.1) | copy-start | bytes 6148
  100.2 11.1 %copy-start.4 = (s32[512,15]{0,1:T(8,128)S(1)}, s32[512,15]{0,1:T(8,128)}, u32[]{:S(2)}) copy-start(s32[512,15]{0,1:T(8,128)} %param.24) | copy-start | bytes 92164
  107.8 12.2 %all-to-all-start.3 = ((bf16[16,32,153]{2,1,0:T(8,128)(2,1)}), bf16[16,32,153]{2,1,0:T(8,128)(2,1)S(1)}, u32[]{:S(2)}, u32[]{:S(2)}) async-start(bf16[16,32,153]{2,1,0:T(8,128)(2,1)} %bitcast.7), calls=%async_computation.3 | async-start | bytes 524288 | tf_op jit(solution)/shard_map/all_to_all | solution.py:382

commit v6 on v5

--- a/solution.py
+++ b/solution.py
@@ -54,8 +54,10 @@
 
 
 def select_rows_kernel(idx_hbm, table_hbm, out_hbm, idx_ref, table_ref, out_ref, idx_sem, table_sem, out_sem):
-    blocks = out_ref.shape[0] // BLOCK
-    at = [pl.ds(b * BLOCK, BLOCK) for b in range(blocks)]
+    rows = out_ref.shape[0]
+    at = [pl.ds(b, BLOCK) for b in range(0, rows - BLOCK, BLOCK)]
+    at += [pl.ds(rows - BLOCK, BLOCK // 2), pl.ds(rows - BLOCK // 2, BLOCK // 2)]
+    blocks = len(at)
     idx_in = pltpu.make_async_copy(idx_hbm, idx_ref, idx_sem)
     table_in = pltpu.make_async_copy(table_hbm, table_ref, table_sem)
     copies = [pltpu.make_async_copy(out_ref.at[at[b]], out_hbm.at[at[b]], out_sem.at[b]) for b in range(blocks)]
@@ -85,7 +87,7 @@
             pltpu.VMEM((rows, width), bf16),
             pltpu.SemaphoreType.DMA,
             pltpu.SemaphoreType.DMA,
-            pltpu.SemaphoreType.DMA((rows // BLOCK,)),
+            pltpu.SemaphoreType.DMA((rows // BLOCK + 1,)),
         ],
         compiler_params=params(24),
         name="select_rows",
@@ -142,7 +144,7 @@
     rows, width = hot_ref.shape
     blocks = rows // BLOCK
     at = [pl.ds(b * BLOCK, BLOCK) for b in range(blocks)]
-    out = at[:-1] + [pl.ds(rows - BLOCK, BLOCK // 2), pl.ds(rows - BLOCK // 2, BLOCK // 2)]
+    out = at[:-1] + [pl.ds(rows - BLOCK + c * LANES, LANES) for c in range(BLOCK // LANES)]
     hot_in = pltpu.make_async_copy(hot_hbm, hot_ref, hot_sem)
     adj_in = pltpu.make_async_copy(adj_hbm, adj_ref, adj_sem)
     ws_in = pltpu.make_async_copy(ws_hbm, w_ref.at[pl.ds(0, width)], ws_sem)
@@ -199,7 +201,7 @@
             pltpu.SemaphoreType.DMA,
             pltpu.SemaphoreType.DMA,
             pltpu.SemaphoreType.DMA,
-            pltpu.SemaphoreType.DMA((blocks + 1,)),
+            pltpu.SemaphoreType.DMA((blocks - 1 + BLOCK // LANES,)),
             pltpu.VMEM((rows, 2 * width), bf16),
         ],
         compiler_params=params(48),

time: 122 us -> 121 us (level)
  no operation moved by 1% of the time
where the time goes in v6:
time: 121 us
  Pallas kernels  59 us (49%)
  blocking collectives  19.9 us (16%)
  local copies, waits for them, and re-layouts  15.3 us (13%)
  starting transfers between devices  14.7 us (12%)
  waiting for transfers between devices  11.7 us (10%)
    pallas_call x1, Pallas kernels, first_layer(): pl.pallas_call(functools.partial(first_layer_kernel, fanout=fanout), in_s...  22.6 us
    all_to_all x2, blocking collectives, sum_over(): lax.all_to_all(copies, axes, split_axis=0, concat_axis=0, tiled=True)  19.9 us
    pallas_call x1, Pallas kernels, counts(): pl.pallas_call(count_neighbours, grid=(rows // block,), in_specs=[pl.Bloc...  16.7 us
    gather x1, local copies, waits for them, and re-layouts, local(): hot_feat = hot_rows.at[hot_id].get(mode='promise_in_bounds')  13.7 us
    all_to_all x1, starting transfers between devices, local(): lax.all_to_all(outgoing, HST_DEV, split_axis=0, concat_axis=0, tiled=True)  11.2 us
    all_to_all x1, waiting for transfers between devices, local(): lax.all_to_all(outgoing, HST_DEV, split_axis=0, concat_axis=0, tiled=True)  8.54 us
    pallas_call x1, Pallas kernels, second_layer(): pl.pallas_call(functools.partial(second_layer_kernel, total_rows=total_ro...  7.54 us
    pallas_call x1, Pallas kernels, select_rows(): pl.pallas_call(select_rows_kernel, in_specs=[HBM, HBM], out_specs=HBM, ou...  5.7 us
  transfers between devices with their start and end apart: 2, of which 2 were waited for; matrix products, arithmetic and copies ran while one was open for 13% of the time, Pallas kernels for 18%

profile of v6, /device:TPU:0, one launch (start us, length us, event | category | flops | bytes accessed | tf_op | source)
XLA Modules:
  0.0 120.9 jit_solution(10918092617023573864)
XLA Ops:
  0.0 5.7 %select_rows.1 = bf16[2048,768]{1,0:T(8,128)(2,1)} custom-call(s32[1,2048]{1,0:T(1,128)} %idx_hbm.1, bf16[1024,768]{1,0:T(8,128)(2,1)} %table_hbm.1), custom_call_target="tpu_custom_call" | custom-call | tf_op jit(solution)/shard_map/select_rows/pallas_call | solution.py:79
  5.7 0.0 copy-start.3
  5.7 0.0 copy-start.5
  5.7 11.2 %all-to-all-start = ((bf16[128,16,768]{2,1,0:T(8,128)(2,1)}), bf16[128,16,768]{2,1,0:T(8,128)(2,1)S(1)}, u32[]{:S(2)}, u32[]{:S(2)}) async-start(bf16[128,16,768]{2,1,0:T(8,128)(2,1)} %bitcast.15), calls=%async_computation | async-start | bytes 6291456 | tf_op jit(solution)/shard_map/all_to_all | solution.py:366
  16.9 0.0 copy-done.3
  16.9 1.4 %copy.21.adj_ref = s32[2048,15]{1,0:T(8,128)} copy(s32[2048,15]{0,1:T(8,128)S(1)} %copy-done.3) | data formatting | bytes 245760 | tf_op args[7]
  18.3 0.0 copy-done.5
  18.3 13.7 %gather_fusion = bf16[2048,768]{1,0:T(8,128)(2,1)} fusion(bf16[4096,768]{1,0:T(8,128)(2,1)} %param.16, s32[2048]{0:T(1024)S(1)} %fusion), kind=kCustom, calls=%fused_computation | custom fusion | bytes 6299648 | tf_op jit(solution)/shard_map/gather | solution.py:368
  32.0 0.0 copy-start.6
  32.0 0.0 copy-start.7
  32.0 0.0 copy-start.8
  32.0 16.7 %neighbour_counts.1.adj_hbm = bf16[2048,2048]{1,0:T(8,128)(2,1)} custom-call(s32[2048,15]{1,0:T(8,128)} %copy.21.adj_ref), custom_call_target="tpu_custom_call" | custom-call | flops 188743680 | bytes 8388608 | tf_op jit(solution)/shard_map/neighbour_counts/pallas_call | solution.py:126
  48.7 0.0 copy-done.6
  48.7 0.0 copy-done.7
  48.7 0.0 copy-done.8
  48.7 8.5 %all-to-all-done = bf16[128,16,768]{2,1,0:T(8,128)(2,1)S(1)} async-done(((bf16[128,16,768]{2,1,0:T(8,128)(2,1)}), bf16[128,16,768]{2,1,0:T(8,128)(2,1)S(1)}, u32[]{:S(2)}, u32[]{:S(2)}) %all-to-all-start) | async-done | bytes 3145760 | tf_op jit(solution)/shard_map/all_to_all | solution.py:366
  57.3 0.0 copy-start
  57.3 0.0 copy-start.1
  57.3 0.0 copy-start.2
  57.3 22.6 %first_layer.1 = (f32[2048,1024]{1,0:T(8,128)}, f32[2,1024]{1,0:T(2,128)S(1)}) custom-call(s32[1,2048]{1,0:T(1,128)S(1)} %bitcast.12, bf16[2048,768]{1,0:T(8,128)(2,1)S(1)} %bitcast.10, bf16[2048,768]{1,0:T(8,128)(2,1)} %gather_fusion, bf16[2048,2048]{1,0:T(8,128)(2,1)} %neighbour_counts.1.adj_hbm, bf16[768,1024]{1,0:T(8,128)(2,1)} %ws_hbm.1, ...), custom_call_target="tpu_custom_call" | custom-call | tf_op jit(solution)/shard_map/first_layer/pallas_call | solution.py:187
  79.9 8.5 %all_to_all.32 = f32[8,2,1024]{2,1,0:T(2,128)S(1)} all-to-all(f32[8,2,1024]{2,1,0:T(2,128)S(1)} %broadcast_in_dim.31), channel_id=1, replica_groups=mesh['hst_0'=4,'hst_1'=2,'dev_0'=4,'dev_1'=4] {'hst_0','hst_1'}, dimensions={0} | all-to-all | bytes 131072 | tf_op jit(solution)/shard_map/all_to_all | solution.py:339
  88.5 11.4 %all_to_all.33 = f32[16,2,1024]{2,1,0:T(2,128)S(1)} all-to-all(f32[16,2,1024]{2,1,0:T(2,128)S(1)} %broadcast_in_dim.32), channel_id=1, replica_groups=mesh['hst_0'=4,'hst_1'=2,'dev_0'=4,'dev_1'=4] {'dev_0','dev_1'}, dimensions={0} | all-to-all | bytes 262144 | tf_op jit(solution)/shard_map/all_to_all | solution.py:339
  99.9 0.1 reduce_sum.19.stat_ref
  100.0 0.0 copy-done
  100.0 0.0 copy-done.1
  100.0 0.0 copy-done.2
  100.0 0.0 copy-start.4
  100.0 7.5 %second_layer.1 = (f32[512,153]{1,0:T(8,128)}, bf16[2048,153]{1,0:T(8,128)(2,1)}, bf16[512,153]{1,0:T(8,128)(2,1)}) custom-call(f32[2048,1024]{1,0:T(8,128)} %get-tuple-element.12.pre_hbm, f32[2,1024]{1,0:T(2,128)S(1)} %reduce_sum.19.stat_ref, f32[1,1024]{1,0:T(1,128)S(1)} %bitcast.13, f32[1,1024]{1,0:T(1,128)S(1)} %bitcast.14, s32[1,512]{1,0:T(1,128)S(1)} %copy-done.2, ...), custom_call_target="tpu_custom_call" | custom-call | tf_op jit(solution)/shard_map/second_layer/pallas_call | solution.py:259
  107.6 3.5 %all-to-all-start.3 = ((bf16[16,32,153]{2,1,0:T(8,128)(2,1)}), bf16[16,32,153]{2,1,0:T(8,128)(2,1)S(1)}, u32[]{:S(2)}, u32[]{:S(2)}) async-start(bf16[16,32,153]{2,1,0:T(8,128)(2,1)} %bitcast.7), calls=%async_computation.3 | async-start | bytes 524288 | tf_op jit(solution)/shard_map/all_to_all | solution.py:384
  111.1 0.0 copy-done.4
  111.1 0.1 copy.24.adj_ref
  111.3 5.3 %targets_layer.1 = (f32[512,153]{1,0:T(8,128)S(1)}, bf16[512,512]{1,0:T(8,128)(2,1)S(1)}) custom-call(s32[512,15]{1,0:T(8,128)S(1)} %copy.24.adj_ref, f32[512,153]{1,0:T(8,128)} %get-tuple-element.14.own_hbm, bf16[2048,153]{1,0:T(8,128)(2,1)} %get-tuple-element.15.neigh_hbm), custom_call_target="tpu_custom_call" | custom-call | flops 58982400 | bytes 2097152 | tf_op jit(solution)/shard_map/targets_layer/pallas_call | solution.py:301
  116.6 3.2 %all-to-all-done.3 = bf16[16,32,153]{2,1,0:T(8,128)(2,1)S(1)} async-done(((bf16[16,32,153]{2,1,0:T(8,128)(2,1)}), bf16[16,32,153]{2,1,0:T(8,128)(2,1)S(1)}, u32[]{:S(2)}, u32[]{:S(2)}) %all-to-all-start.3) | async-done | bytes 156704 | tf_op jit(solution)/shard_map/all_to_all | solution.py:384
  119.8 1.1 output_layer.1
  (5 shorter events, 0.1 us)
Async XLA Ops:
  5.7 11.2 %copy-start.3 = (s32[2048,15]{0,1:T(8,128)S(1)}, s32[2048,15]{0,1:T(8,128)}, u32[]{:S(2)}) copy-start(s32[2048,15]{0,1:T(8,128)} %param.23) | copy-start | bytes 368644
  5.7 12.6 %copy-start.5 = (s32[2048]{0:T(1024)S(1)}, s32[2048]{0:T(1024)}, u32[]{:S(2)}) copy-start(s32[2048]{0:T(1024)} %param.19) | copy-start | bytes 24580
  5.7 51.6 %all-to-all-start = ((bf16[128,16,768]{2,1,0:T(8,128)(2,1)}), bf16[128,16,768]{2,1,0:T(8,128)(2,1)S(1)}, u32[]{:S(2)}, u32[]{:S(2)}) async-start(bf16[128,16,768]{2,1,0:T(8,128)(2,1)} %bitcast.15), calls=%async_computation | async-start | bytes 6291456 | tf_op jit(solution)/shard_map/all_to_all | solution.py:366
  32.0 16.7 %copy-start.6 = (s32[2048]{0:T(1024)S(1)}, s32[2048]{0:T(1024)}, u32[]{:S(2)}) copy-start(s32[2048]{0:T(1024)} %param.21) | copy-start | bytes 24580
  32.0 16.7 %copy-start.7 = (s32[2048]{0:T(1024)S(1)}, s32[2048]{0:T(1024)}, u32[]{:S(2)}) copy-start(s32[2048]{0:T(1024)} %param.20) | copy-start | bytes 24580
  32.0 16.7 %copy-start.8 = (s32[2048]{0:T(1024)S(1)}, s32[2048]{0:T(1024)}, u32[]{:S(2)}) copy-start(s32[2048]{0:T(1024)} %param.18) | copy-start | bytes 24580
  57.3 42.7 %copy-start = (f32[1024]{0:T(1024)S(1)}, f32[1024]{0:T(1024)}, u32[]{:S(2)}) copy-start(f32[1024]{0:T(1024)} %param.28) | copy-start | bytes 12292
  57.3 42.7 %copy-start.1 = (f32[1024]{0:T(1024)S(1)}, f32[1024]{0:T(1024)}, u32[]{:S(2)}) copy-start(f32[1024]{0:T(1024)} %param.29) | copy-start | bytes 12292
  57.3 42.7 %copy-start.2 = (s32[1,512]{1,0:T(1,128)S(1)}, s32[1,512]{1,0:T(1,128)}, u32[]{:S(2)}) copy-start(s32[1,512]{1,0:T(1,128)} %send_ref.1) | copy-start | bytes 6148
  100.0 11.1 %copy-start.4 = (s32[512,15]{0,1:T(8,128)S(1)}, s32[512,15]{0,1:T(8,128)}, u32[]{:S(2)}) copy-start(s32[512,15]{0,1:T(8,128)} %param.24) | copy-start | bytes 92164
  107.6 12.2 %all-to-all-start.3 = ((bf16[16,32,153]{2,1,0:T(8,128)(2,1)}), bf16[16,32,153]{2,1,0:T(8,128)(2,1)S(1)}, u32[]{:S(2)}, u32[]{:S(2)}) async-start(bf16[16,32,153]{2,1,0:T(8,128)(2,1)} %bitcast.7), calls=%async_computation.3 | async-start | bytes 524288 | tf_op jit(solution)/shard_map/all_to_all | solution.py:384
